TPU v7x, 128 devices: a whole 4x4x4 slice. The times are simulated.
128 devices in a mesh: grp: 8 (over y_hi, z), pair: 16 (over x, y_lo, core).
Axes of the slice: x: 4, y: 4 (y_hi: 2, y_lo: 2; y = y_hi * 2 + y_lo), z: 4, core: 2. Of those that a mesh axis runs over, the one named last changes fastest.
Arguments:
- amplitudes: bfloat16 [128, 512, 512], P('pair', 'grp'), may hold values from -6 to 6
- cholesky: bfloat16 [512, 512, 2048], P('pair', 'grp'), may hold values from -0.09375 to 0.09375
Outputs:
- ladder_term: float32 [512, 4, 128], P('pair', None, 'grp')
All inputs are finite; a program needn't handle non-finite values.
Results may differ from a plain program's by a relative error of at most 0.003.
Values may be sent and summed in bfloat16 or wider, within the bound.
No kernel may reach another device: no remote copies, remote signals or barrier semaphores. Data moves between devices by JAX's collectives and lax.ppermute only.
A program may use at most 128 MiB of HBM per device.

v0:
```python
import functools

import jax
import jax.numpy as jnp
from jax import lax
from jax.experimental import pallas as pl
from jax.experimental.pallas import tpu as pltpu
from jax.sharding import PartitionSpec as P


AXES = ("grp", "pair")
DT = 16
VMEM_MIB = 48


def linear(x, y, z, c):
    return ((y // 2) * 4 + z) * 16 + (x * 2 + y % 2) * 2 + c


def moved(value, where):
    pairs = []
    for x in range(4):
        for y in range(4):
            for z in range(4):
                for c in range(2):
                    to = where(x, y, z, c)
                    if to is not None:
                        pairs.append(
                            (linear(x, y, z, c), linear(to[0] % 4, to[1] % 4, to[2] % 4, to[3]))
                        )
    return lax.ppermute(value, AXES, pairs)


def position():
    g, p = lax.axis_index("grp"), lax.axis_index("pair")
    return p // 4, (g // 4) * 2 + (p // 2) % 2, g % 4, p % 2


def gathered_window(cholesky, x, y, k):
    at_root = lambda x, y, c: x == 0 and y % 2 == 0 and c == 0
    got = [
        moved(cholesky[dx], lambda x, y, z, c: (dx, y, z, y // 2) if at_root(x, y, c) else None)
        for dx in (1, 3, 2)
    ]
    got.append(
        moved(cholesky[0], lambda x, y, z, c: (0, y, z, 1) if at_root(x, y, c) and y == 2 else None)
    )
    own = jnp.where((x == 0) & (y == 0) & (k == 0), cholesky[0], jnp.zeros_like(cholesky[0]))
    piece = own + got[0] + got[1] + got[2] + got[3]
    spread = [
        moved(piece, lambda x, y, z, c: (x, y + dy, z, c) if y == 2 * c else None)
        for dy in (1, 3, 2)
    ]
    piece = piece + spread[0] + spread[1] + spread[2]
    others = [moved(piece, lambda x, y, z, c: (x - dx, y, z, c)) for dx in (1, 3, 2)]
    early = [moved(piece, lambda x, y, z, c: (x, y, z - j, c)) for j in (1, 3, 2)]
    half = others[2].shape[0] // 2
    upper = jnp.concatenate([others[0], others[2][:half]])
    lower = jnp.concatenate([others[2][half:], others[1]])
    rise = lambda x, y, z, c: (x, y, z + 1, c)
    fall = lambda x, y, z, c: (x, y, z - 1, c)
    up, down = moved(upper, rise), moved(lower, fall)
    up_more, down_more = moved(lower, rise), moved(upper, fall)
    up_far, down_far = moved(up, rise), moved(down, fall)
    return [
        [piece, upper, lower],
        [early[0], down_more, down],
        [early[2], up_far, down_far],
        [early[1], up, up_more],
    ]


def gathered_amplitudes(amplitudes, z, k):
    n_ij, n_d = amplitudes.shape[:2]
    parts = amplitudes.reshape(n_ij, n_d, 2, 4, 64).transpose(2, 3, 0, 1, 4).reshape(2, 4, n_ij, n_d * 64)
    twice = jnp.concatenate([parts, parts], axis=1)
    turned = lax.dynamic_slice_in_dim(twice, z, 4, 1)
    mine = lax.dynamic_index_in_dim(turned, k, 0, keepdims=False)
    other = lax.dynamic_index_in_dim(turned, 1 - k, 0, keepdims=False)
    came = moved(other, lambda x, y, z, c: (x, y, z, 1 - c))
    a0 = jnp.concatenate([mine, came], axis=1)
    across = lambda x, y, z, c: (x, y ^ 1, z, c)
    b0 = moved(a0, across)
    a1, a3, a2 = [moved(a0, lambda x, y, z, c: (x - dx, y, z, c)) for dx in (1, 3, 2)]
    b1, b3 = [moved(b0, lambda x, y, z, c: (x - dx, y, z, c)) for dx in (1, 3)]
    b2 = moved(a2, across)
    return [a0, b0, a1, b1, a2, b2, a3, b3]


NT = (((1,), (1,)), ((), ()))


def kernel(counts, stored, emit, last, pos_ref, *refs):
    blocks = len(counts)
    x_refs, refs = refs[:2], refs[2:]
    w_refs = []
    for count in counts:
        w_refs.append(refs[:count])
        refs = refs[count:]
    total_blocks = 0 if emit else blocks + stored
    t_refs, refs = refs[: 8 * total_blocks], refs[8 * total_blocks :]
    s_refs, refs = refs[:stored], refs[stored:]
    o_ref, wbuf, tile, total = refs[-4:]
    acc_ref = refs[0] if len(refs) > 4 else None
    step = pl.program_id(0)

    @pl.when(step == 0)
    def _():
        row = 0
        for pieces in w_refs:
            for w_ref in pieces:
                wbuf[row : row + w_ref.shape[0]] = w_ref[...]
                row += w_ref.shape[0]
        if not emit:
            total[...] = jnp.zeros_like(total) if acc_ref is None else acc_ref[...]

    for h in range(2):
        rows = x_refs[h][...].reshape(DT * 32, -1)
        product = lax.dot_general(rows, wbuf[...], NT, preferred_element_type=jnp.float32)
        for lane in range(2 * blocks):
            tile[h, lane] = product[:, 128 * lane : 128 * (lane + 1)]

    def regrouped(n, q, h, a):
        lane, at = 2 * n + a // 2, (a % 2) * 64
        parts = [
            tile[h, lane, pl.ds(4 * q + d, 32, stride=DT), :][:, at : at + 64].astype(jnp.bfloat16)
            for d in range(4)
        ]
        return jnp.concatenate(parts, axis=1)

    for q in range(DT // 4):
        lefts = []
        for n in range(blocks):
            group = [regrouped(n, q, h, a) for h in range(2) for a in range(4)]
            lefts.append(jnp.concatenate(group, axis=0))
        if emit:
            for n in range(blocks):
                o_ref[n, q] = lefts[n]
            continue
        lefts += [s_ref[0, q] for s_ref in s_refs]
        for n in range(total_blocks):
            amp = jnp.concatenate(
                [t_refs[8 * n + r][0, :, 256 * q : 256 * (q + 1)] for r in range(8)], axis=0
            )
            total[...] += lax.dot_general(amp, lefts[n], NT, preferred_element_type=jnp.float32)

    if emit:
        return

    @pl.when(step == pl.num_programs(0) - 1)
    def _():
        if last:
            x, low, k = pos_ref[0], pos_ref[1], pos_ref[2]
            for dx in range(4):
                for dy in range(2):
                    to = lax.rem(x + dx, 4) * 2 + (low + dy) % 2
                    for e in range(2):
                        row = (dx * 2 + dy) * 16 + e * 8
                        o_ref[to, (k + e) % 2] = total[row : row + 8, :]
        else:
            o_ref[...] = total[...]


def contracted(pos, chol, window, amps, js, acc=None, stored=(), emit=False, last=False):
    blocks = len(js)
    n_d = chol[0].shape[1]
    full = lambda shape: pl.BlockSpec(shape, lambda i, pos: (0,) * len(shape))
    in_specs = [pl.BlockSpec((32, DT, 2048), lambda i, pos: (0, i, 0))] * 2
    operands = list(chol)
    for j in js:
        in_specs += [full(piece.shape) for piece in window[j]]
        operands += window[j]
    if not emit:
        for j in [*js, *(j for j, _, _ in stored)]:
            in_specs += [pl.BlockSpec((1, 16, DT * 64), lambda i, pos, j=j: (j, 0, i))] * 8
            operands += amps
    for _, left, n in stored:
        in_specs.append(pl.BlockSpec((1, DT // 4, 256, 256), lambda i, pos, n=n: (n, i, 0, 0)))
        operands.append(left)
    if acc is not None:
        in_specs.append(full((128, 256)))
        operands.append(acc)
    if emit:
        out = jax.ShapeDtypeStruct((blocks, n_d // 4, 256, 256), jnp.bfloat16)
        out_specs = pl.BlockSpec((blocks, DT // 4, 256, 256), lambda i, pos: (0, i, 0, 0))
    else:
        out = jax.ShapeDtypeStruct((8, 2, 8, 256) if last else (128, 256), jnp.float32)
        out_specs = full(out.shape)
    return pl.pallas_call(
        functools.partial(kernel, [len(window[j]) for j in js], len(stored), emit, last),
        grid_spec=pltpu.PrefetchScalarGridSpec(
            num_scalar_prefetch=1,
            grid=(n_d // DT,),
            in_specs=in_specs,
            out_specs=out_specs,
            scratch_shapes=[
                pltpu.VMEM((256 * blocks, 2048), jnp.bfloat16),
                pltpu.VMEM((2, 2 * blocks, DT * 32, 128), jnp.float32),
                pltpu.VMEM((128, 256), jnp.float32),
            ],
        ),
        out_shape=out,
        compiler_params=pltpu.CompilerParams(vmem_limit_bytes=VMEM_MIB * 1024 * 1024),
        cost_estimate=pl.CostEstimate(
            flops=blocks * 2 * 4096 * 256 * 2048, bytes_accessed=20 * 1024 * 1024, transcendentals=0
        ),
    )(pos, *operands)


def per_device(amplitudes, cholesky):
    x, y, z, k = position()
    pos = jnp.stack([x, y % 2, k]).astype(jnp.int32)
    swap = lambda x, y, z, c: (x, y, z, 1 - c)
    chol = (cholesky, moved(cholesky, swap))
    window = gathered_window(cholesky, x, y, k)
    amps = gathered_amplitudes(amplitudes, z, k)
    first = contracted(pos, chol, window, amps, (0,), emit=True)
    second = contracted(pos, chol, window, amps, (1, 3), emit=True)
    stored = ((0, first, 0), (1, second, 0), (3, second, 1))
    acc = contracted(pos, chol, window, amps, (2,), stored=stored, last=True)
    parts = acc.reshape(8, 16, 256)
    own = parts[:, :, :128] + moved(parts[:, :, 128:], swap)
    blocks = lax.all_to_all(own, "grp", 0, 0, tiled=True)
    result = jnp.sum(blocks, axis=0).reshape(16, 4, 32)
    result = lax.dynamic_slice_in_dim(jnp.concatenate([result, result], axis=1), (4 - x) % 4, 4, 1)
    return result.transpose(2, 1, 0)


def solution(mesh):
    in_specs = (P("pair", "grp", None), P("pair", "grp", None))
    out_specs = P("pair", None, "grp")
    return jax.shard_map(
        per_device, mesh=mesh, in_specs=in_specs, out_specs=out_specs, check_vma=False
    )
```

profile of v0, /device:TPU:0, one launch (start us, length us, event | category | flops | bytes accessed | tf_op | source)
XLA Modules:
  0.0 152.2 jit_solution(3403334332544580483)
XLA Ops:
  0.0 2.2 %slice_bitcast_fusion.2 = (bf16[64,2048]{1,0:T(8,128)(2,1)}, bf16[64,2048]{1,0:T(8,128)(2,1)}, bf16[64,2048]{1,0:T(8,128)(2,1)}, bf16[64,2048]{1,0:T(8,128)(2,1)}) fusion(bf16[32,64,2048]{2,1,0:T(8,128)(2,1)} %refs_0_.5), kind=kLoop, calls=%fused_computation.9 | loop fusion | bytes 2097152 | tf_op jit(solution)/shard_map/squeeze | solution.py:42
  2.2 3.5 %collective-permute-start.1 = (bf16[64,2048]{1,0:T(8,128)(2,1)}, bf16[64,2048]{1,0:T(8,128)(2,1)S(1)}, u32[]{:S(2)}, u32[]{:S(2)}) collective-permute-start(bf16[64,2048]{1,0:T(8,128)(2,1)} %get-tuple-element.5), channel_id=1, source_target_pairs={{0,4},{16,20},{32,36},{48,52},{64,69},{80,85},{96,101},{112,117}} | collective-permute-start | bytes 786440 | tf_op jit(solution)/shard_map/ppermute | solution.py:31
  5.7 1.9 %collective-permute-start.2 = (bf16[64,2048]{1,0:T(8,128)(2,1)}, bf16[64,2048]{1,0:T(8,128)(2,1)S(1)}, u32[]{:S(2)}, u32[]{:S(2)}) collective-permute-start(bf16[64,2048]{1,0:T(8,128)(2,1)} %get-tuple-element.7), channel_id=1, source_target_pairs={{0,12},{16,28},{32,44},{48,60},{64,77},{80,93},{96,109},{112,125}} | collective-permute-start | bytes 786440 | tf_op jit(solution)/shard_map/ppermute | solution.py:31
  10.4 2.2 %reshape.12 = bf16[8,64,2,4,64]{4,3,2,1,0:T(4,128)(2,1)S(1)} reshape(bf16[8,64,512]{2,1,0:T(8,128)(2,1)} %param.2) | data formatting | bytes 1048576 | tf_op jit(solution)/shard_map/reshape | solution.py:75
  17.5 4.6 %collective-permute-start.7 = (bf16[64,2048]{1,0:T(8,128)(2,1)S(1)}, bf16[64,2048]{1,0:T(8,128)(2,1)S(1)}, u32[]{:S(2)}, u32[]{:S(2)}) collective-permute-start(bf16[64,2048]{1,0:T(8,128)(2,1)S(1)} %add_add_fusion.1), channel_id=1, source_target_pairs={{0,64},{16,80},{32,96},{48,112},{65,1},{81,17},{97,33},{113,49},{4... | collective-permute-start | bytes 786440 | tf_op jit(solution)/shard_map/ppermute | solution.py:31
  22.3 3.7 %collective-permute-done.7 = bf16[64,2048]{1,0:T(8,128)(2,1)S(1)} collective-permute-done((bf16[64,2048]{1,0:T(8,128)(2,1)S(1)}, bf16[64,2048]{1,0:T(8,128)(2,1)S(1)}, u32[]{:S(2)}, u32[]{:S(2)}) %collective-permute-start.7) | collective-permute-done | bytes 262176 | tf_op jit(solution)/shard_map/ppermute | solution.py:31
  26.3 3.2 %collective-permute-start.9 = (bf16[64,2048]{1,0:T(8,128)(2,1)S(1)}, bf16[64,2048]{1,0:T(8,128)(2,1)S(1)}, u32[]{:S(2)}, u32[]{:S(2)}) collective-permute-start(bf16[64,2048]{1,0:T(8,128)(2,1)S(1)} %add_add_fusion.refs_2_), channel_id=1, source_target_pairs={{0,12},{1,13},{16,28},{17,29},{32,44},{33,45},{48,60},{49,61},{2,1... | collective-permute-start | bytes 786440 | tf_op jit(solution)/shard_map/ppermute | solution.py:31
  29.7 7.2 %collective-permute-done.10 = bf16[64,2048]{1,0:T(8,128)(2,1)S(1)} collective-permute-done((bf16[64,2048]{1,0:T(8,128)(2,1)S(1)}, bf16[64,2048]{1,0:T(8,128)(2,1)S(1)}, u32[]{:S(2)}, u32[]{:S(2)}) %collective-permute-start.10) | collective-permute-done | bytes 262176 | tf_op jit(solution)/shard_map/ppermute | solution.py:31
  36.9 5.3 %collective-permute-done.13 = bf16[64,2048]{1,0:T(8,128)(2,1)S(1)} collective-permute-done((bf16[64,2048]{1,0:T(8,128)(2,1)S(1)}, bf16[64,2048]{1,0:T(8,128)(2,1)S(1)}, u32[]{:S(2)}, u32[]{:S(2)}) %collective-permute-start.13) | collective-permute-done | bytes 262176 | tf_op jit(solution)/shard_map/ppermute | solution.py:31
  43.0 4.0 %collective-permute-start.24 = (bf16[64,2048]{1,0:T(8,128)(2,1)S(1)}, bf16[64,2048]{1,0:T(8,128)(2,1)S(1)}, u32[]{:S(2)}, u32[]{:S(2)}) collective-permute-start(bf16[64,2048]{1,0:T(8,128)(2,1)S(1)} %add_add_fusion.refs_2_), channel_id=1, source_target_pairs={{0,48},{1,49},{16,0},{17,1},{32,16},{33,17},{48,32},{49,33},{2,50}... | collective-permute-start | bytes 786440 | tf_op jit(solution)/shard_map/ppermute | solution.py:31
  47.1 5.0 %collective-permute-done.24.refs_2_ = bf16[64,2048]{1,0:T(8,128)(2,1)S(1)} collective-permute-done((bf16[64,2048]{1,0:T(8,128)(2,1)S(1)}, bf16[64,2048]{1,0:T(8,128)(2,1)S(1)}, u32[]{:S(2)}, u32[]{:S(2)}) %collective-permute-start.24) | collective-permute-done | bytes 262176 | tf_op jit(solution)/shard_map/ppermute | solution.py:31
  53.4 8.0 %collective-permute-done.26.refs_5_ = bf16[64,2048]{1,0:T(8,128)(2,1)S(1)} collective-permute-done((bf16[64,2048]{1,0:T(8,128)(2,1)S(1)}, bf16[64,2048]{1,0:T(8,128)(2,1)S(1)}, u32[]{:S(2)}, u32[]{:S(2)}) %collective-permute-start.26) | collective-permute-done | bytes 262176 | tf_op jit(solution)/shard_map/ppermute | solution.py:31
  62.1 1.7 %collective-permute-start.14 = (bf16[96,2048]{1,0:T(8,128)(2,1)S(1)}, bf16[96,2048]{1,0:T(8,128)(2,1)S(1)}, u32[]{:S(2)}, u32[]{:S(2)}) collective-permute-start(bf16[96,2048]{1,0:T(8,128)(2,1)S(1)} %pad_maximum_fusion.2.refs_4_), channel_id=1, source_target_pairs={{0,48},{1,49},{16,0},{17,1},{32,16},{33,17},{48,32},{49,33},{2,50}... | collective-permute-start | bytes 1179656 | tf_op jit(solution)/shard_map/ppermute | solution.py:31
  64.2 3.2 %collective-permute-start.25 = (bf16[96,2048]{1,0:T(8,128)(2,1)S(1)}, bf16[96,2048]{1,0:T(8,128)(2,1)}, u32[]{:S(2)}, u32[]{:S(2)}) collective-permute-start(bf16[96,2048]{1,0:T(8,128)(2,1)S(1)} %pad_maximum_fusion.1.refs_3_), channel_id=1, source_target_pairs={{0,48},{1,49},{16,0},{17,1},{32,16},{33,17},{48,32},{49,33},{2,50}... | collective-permute-start | bytes 1179656 | tf_op jit(solution)/shard_map/ppermute | solution.py:31
  67.4 6.6 %collective-permute-done.14.refs_4_ = bf16[96,2048]{1,0:T(8,128)(2,1)S(1)} collective-permute-done((bf16[96,2048]{1,0:T(8,128)(2,1)S(1)}, bf16[96,2048]{1,0:T(8,128)(2,1)S(1)}, u32[]{:S(2)}, u32[]{:S(2)}) %collective-permute-start.14) | collective-permute-done | bytes 393248 | tf_op jit(solution)/shard_map/ppermute | solution.py:31
  74.0 2.3 %collective-permute-start.22 = (bf16[4,16,4096]{2,1,0:T(8,128)(2,1)S(1)}, bf16[4,16,4096]{2,1,0:T(8,128)(2,1)S(1)}, u32[]{:S(2)}, u32[]{:S(2)}) collective-permute-start(bf16[4,16,4096]{2,1,0:T(8,128)(2,1)S(1)} %pad_maximum_fusion.refs_5_.refs_13_.refs_21_.refs_29_), channel_id=1, source_target_pairs={{0,4},{1,5},{16,20},{17,21},{32,36},{33,37},{48,52},{49,53},{2,6},... | collective-permute-start | bytes 1572872 | tf_op jit(solution)/shard_map/ppermute | solution.py:31
  77.5 9.9 %collective-permute-done.11.refs_6_ = bf16[96,2048]{1,0:T(8,128)(2,1)} collective-permute-done((bf16[96,2048]{1,0:T(8,128)(2,1)S(1)}, bf16[96,2048]{1,0:T(8,128)(2,1)}, u32[]{:S(2)}, u32[]{:S(2)}) %collective-permute-start.11) | collective-permute-done | bytes 393248 | tf_op jit(solution)/shard_map/ppermute | solution.py:31
  87.5 2.9 %collective-permute-start.23 = (bf16[4,16,4096]{2,1,0:T(8,128)(2,1)S(1)}, bf16[4,16,4096]{2,1,0:T(8,128)(2,1)S(1)}, u32[]{:S(2)}, u32[]{:S(2)}) collective-permute-start(bf16[4,16,4096]{2,1,0:T(8,128)(2,1)S(1)} %collective-permute-done.17.refs_6_.refs_14_.refs_22_.refs_30_), channel_id=1, source_target_pairs={{0,4},{1,5},{16,20},{17,21},{32,36},{33,37},{48,52},{49,53},{2,6},... | collective-permute-start | bytes 1572872 | tf_op jit(solution)/shard_map/ppermute | solution.py:31
  92.2 15.6 %shard_map.29.refs_38_.refs_39_ = bf16[2,16,256,256]{3,2,1,0:T(8,128)(2,1)} custom-call(s32[3]{0:T(128)S(1)} %pad_add_fusion.pos_ref, bf16[32,64,2048]{2,1,0:T(8,128)(2,1)} %refs_0_.5, bf16[32,64,2048]{2,1,0:T(8,128)(2,1)} %collective-permute-done.refs_1_, bf16[64,2048]{1,0:T(8,128)(2,1)S(1)} %copy-done.2, bf16[96,2048]{1,0:T(8,128)(2,1)} %collective-permute-done.25.refs_3_, ...), custom_call_target="tpu_custom_call" | custom-call | flops 8589934592 | bytes 20971520 | tf_op jit(solution)/shard_map/pallas_call | solution.py:189
  107.9 2.0 %collective-permute-start.12 = (bf16[96,2048]{1,0:T(8,128)(2,1)}, bf16[96,2048]{1,0:T(8,128)(2,1)S(1)}, u32[]{:S(2)}, u32[]{:S(2)}) collective-permute-start(bf16[96,2048]{1,0:T(8,128)(2,1)} %collective-permute-done.11.refs_6_), channel_id=1, source_target_pairs={{0,16},{1,17},{16,32},{17,33},{32,48},{33,49},{48,0},{49,1},{2,18}... | collective-permute-start | bytes 1179656 | tf_op jit(solution)/shard_map/ppermute | solution.py:31
  109.9 10.0 %shard_map.28.refs_37_ = bf16[1,16,256,256]{3,2,1,0:T(8,128)(2,1)S(1)} custom-call(s32[3]{0:T(128)S(1)} %pad_add_fusion.pos_ref, bf16[32,64,2048]{2,1,0:T(8,128)(2,1)} %refs_0_.5, bf16[32,64,2048]{2,1,0:T(8,128)(2,1)} %collective-permute-done.refs_1_, bf16[64,2048]{1,0:T(8,128)(2,1)S(1)} %add_add_fusion.refs_2_, ...), custom_call_target="tpu_custom_call" | custom-call | flops 4294967296 | bytes 20971520 | tf_op jit(solution)/shard_map/pallas_call | solution.py:189
  121.3 17.0 %shard_map.30 = f32[8,2,8,256]{3,2,1,0:T(8,128)S(1)} custom-call(s32[3]{0:T(128)S(1)} %pad_add_fusion.pos_ref, bf16[32,64,2048]{2,1,0:T(8,128)(2,1)} %refs_0_.5, bf16[32,64,2048]{2,1,0:T(8,128)(2,1)} %collective-permute-done.refs_1_, bf16[64,2048]{1,0:T(8,128)(2,1)S(1)} %collective-permute-done.8.refs_2_, ...), custom_call_target="tpu_custom_call" | custom-call | flops 4294967296 | bytes 20971520 | tf_op jit(solution)/shard_map/pallas_call | solution.py:189
  140.3 3.3 %all-to-all-start = ((f32[8,16,128]{2,1,0:T(8,128)}), f32[8,16,128]{2,1,0:T(8,128)S(1)}, u32[]{:S(2)}, u32[]{:S(2)}) async-start(f32[8,16,128]{2,1,0:T(8,128)} %slice_add_fusion), calls=%async_computation | async-start | bytes 131072 | tf_op jit(solution)/shard_map/all_to_all | solution.py:223
  143.6 7.8 %all-to-all-done = f32[8,16,128]{2,1,0:T(8,128)S(1)} async-done(((f32[8,16,128]{2,1,0:T(8,128)}), f32[8,16,128]{2,1,0:T(8,128)S(1)}, u32[]{:S(2)}, u32[]{:S(2)}) %all-to-all-start) | async-done | bytes 65568 | tf_op jit(solution)/shard_map/all_to_all | solution.py:223
  (69 shorter events, 18.5 us)
Async XLA Ops:
  0.0 90.3 %collective-permute-start = (bf16[32,64,2048]{2,1,0:T(8,128)(2,1)}, bf16[32,64,2048]{2,1,0:T(8,128)(2,1)}, u32[]{:S(2)}, u32[]{:S(2)}) collective-permute-start(bf16[32,64,2048]{2,1,0:T(8,128)(2,1)} %refs_0_.5), channel_id=1, source_target_pairs={{0,1},{1,0},{16,17},{17,16},{32,33},{33,32},{48,49},{49,48},{2,3},... | collective-permute-start | bytes 25165832 | tf_op jit(solution)/shard_map/ppermute | solution.py:31
  2.2 11.5 %collective-permute-start.1 = (bf16[64,2048]{1,0:T(8,128)(2,1)}, bf16[64,2048]{1,0:T(8,128)(2,1)S(1)}, u32[]{:S(2)}, u32[]{:S(2)}) collective-permute-start(bf16[64,2048]{1,0:T(8,128)(2,1)} %get-tuple-element.5), channel_id=1, source_target_pairs={{0,4},{16,20},{32,36},{48,52},{64,69},{80,85},{96,101},{112,117}} | collective-permute-start | bytes 786440 | tf_op jit(solution)/shard_map/ppermute | solution.py:31
  5.7 8.0 %collective-permute-start.2 = (bf16[64,2048]{1,0:T(8,128)(2,1)}, bf16[64,2048]{1,0:T(8,128)(2,1)S(1)}, u32[]{:S(2)}, u32[]{:S(2)}) collective-permute-start(bf16[64,2048]{1,0:T(8,128)(2,1)} %get-tuple-element.7), channel_id=1, source_target_pairs={{0,12},{16,28},{32,44},{48,60},{64,77},{80,93},{96,109},{112,125}} | collective-permute-start | bytes 786440 | tf_op jit(solution)/shard_map/ppermute | solution.py:31
  17.5 8.5 %collective-permute-start.7 = (bf16[64,2048]{1,0:T(8,128)(2,1)S(1)}, bf16[64,2048]{1,0:T(8,128)(2,1)S(1)}, u32[]{:S(2)}, u32[]{:S(2)}) collective-permute-start(bf16[64,2048]{1,0:T(8,128)(2,1)S(1)} %add_add_fusion.1), channel_id=1, source_target_pairs={{0,64},{16,80},{32,96},{48,112},{65,1},{81,17},{97,33},{113,49},{4... | collective-permute-start | bytes 786440 | tf_op jit(solution)/shard_map/ppermute | solution.py:31
  26.1 10.8 %collective-permute-start.10 = (bf16[64,2048]{1,0:T(8,128)(2,1)S(1)}, bf16[64,2048]{1,0:T(8,128)(2,1)S(1)}, u32[]{:S(2)}, u32[]{:S(2)}) collective-permute-start(bf16[64,2048]{1,0:T(8,128)(2,1)S(1)} %add_add_fusion.refs_2_), channel_id=1, source_target_pairs={{0,8},{1,9},{16,24},{17,25},{32,40},{33,41},{48,56},{49,57},{2,10}... | collective-permute-start | bytes 786440 | tf_op jit(solution)/shard_map/ppermute | solution.py:31
  26.3 15.9 %collective-permute-start.13 = (bf16[64,2048]{1,0:T(8,128)(2,1)S(1)}, bf16[64,2048]{1,0:T(8,128)(2,1)S(1)}, u32[]{:S(2)}, u32[]{:S(2)}) collective-permute-start(bf16[64,2048]{1,0:T(8,128)(2,1)S(1)} %add_add_fusion.refs_2_), channel_id=1, source_target_pairs={{0,4},{1,5},{16,20},{17,21},{32,36},{33,37},{48,52},{49,53},{2,6},... | collective-permute-start | bytes 786440 | tf_op jit(solution)/shard_map/ppermute | solution.py:31
  26.3 16.8 %collective-permute-start.9 = (bf16[64,2048]{1,0:T(8,128)(2,1)S(1)}, bf16[64,2048]{1,0:T(8,128)(2,1)S(1)}, u32[]{:S(2)}, u32[]{:S(2)}) collective-permute-start(bf16[64,2048]{1,0:T(8,128)(2,1)S(1)} %add_add_fusion.refs_2_), channel_id=1, source_target_pairs={{0,12},{1,13},{16,28},{17,29},{32,44},{33,45},{48,60},{49,61},{2,1... | collective-permute-start | bytes 786440 | tf_op jit(solution)/shard_map/ppermute | solution.py:31
  29.6 34.2 %collective-permute-start.17 = (bf16[4,16,4096]{2,1,0:T(8,128)(2,1)S(1)}, bf16[4,16,4096]{2,1,0:T(8,128)(2,1)S(1)}, u32[]{:S(2)}, u32[]{:S(2)}) collective-permute-start(bf16[4,16,4096]{2,1,0:T(8,128)(2,1)S(1)} %pad_maximum_fusion.refs_5_.refs_13_.refs_21_.refs_29_), channel_id=1, source_target_pairs={{0,2},{1,3},{16,18},{17,19},{32,34},{33,35},{48,50},{49,51},{2,0},... | collective-permute-start | bytes 1572872 | tf_op jit(solution)/shard_map/ppermute | solution.py:31
  36.9 27.2 %collective-permute-start.20 = (bf16[4,16,4096]{2,1,0:T(8,128)(2,1)S(1)}, bf16[4,16,4096]{2,1,0:T(8,128)(2,1)S(1)}, u32[]{:S(2)}, u32[]{:S(2)}) collective-permute-start(bf16[4,16,4096]{2,1,0:T(8,128)(2,1)S(1)} %pad_maximum_fusion.refs_5_.refs_13_.refs_21_.refs_29_), channel_id=1, source_target_pairs={{0,8},{1,9},{16,24},{17,25},{32,40},{33,41},{48,56},{49,57},{2,10}... | collective-permute-start | bytes 1572872 | tf_op jit(solution)/shard_map/ppermute | solution.py:31
  42.2 22.0 %collective-permute-start.18 = (bf16[4,16,4096]{2,1,0:T(8,128)(2,1)S(1)}, bf16[4,16,4096]{2,1,0:T(8,128)(2,1)S(1)}, u32[]{:S(2)}, u32[]{:S(2)}) collective-permute-start(bf16[4,16,4096]{2,1,0:T(8,128)(2,1)S(1)} %pad_maximum_fusion.refs_5_.refs_13_.refs_21_.refs_29_), channel_id=1, source_target_pairs={{0,12},{1,13},{16,28},{17,29},{32,44},{33,45},{48,60},{49,61},{2,1... | collective-permute-start | bytes 1572872 | tf_op jit(solution)/shard_map/ppermute | solution.py:31
  43.0 9.0 %collective-permute-start.24 = (bf16[64,2048]{1,0:T(8,128)(2,1)S(1)}, bf16[64,2048]{1,0:T(8,128)(2,1)S(1)}, u32[]{:S(2)}, u32[]{:S(2)}) collective-permute-start(bf16[64,2048]{1,0:T(8,128)(2,1)S(1)} %add_add_fusion.refs_2_), channel_id=1, source_target_pairs={{0,48},{1,49},{16,0},{17,1},{32,16},{33,17},{48,32},{49,33},{2,50}... | collective-permute-start | bytes 786440 | tf_op jit(solution)/shard_map/ppermute | solution.py:31
  52.8 8.6 %collective-permute-start.26 = (bf16[64,2048]{1,0:T(8,128)(2,1)S(1)}, bf16[64,2048]{1,0:T(8,128)(2,1)S(1)}, u32[]{:S(2)}, u32[]{:S(2)}) collective-permute-start(bf16[64,2048]{1,0:T(8,128)(2,1)S(1)} %add_add_fusion.refs_2_), channel_id=1, source_target_pairs={{0,16},{1,17},{16,32},{17,33},{32,48},{33,49},{48,0},{49,1},{2,18}... | collective-permute-start | bytes 786440 | tf_op jit(solution)/shard_map/ppermute | solution.py:31
  62.1 12.0 %collective-permute-start.14 = (bf16[96,2048]{1,0:T(8,128)(2,1)S(1)}, bf16[96,2048]{1,0:T(8,128)(2,1)S(1)}, u32[]{:S(2)}, u32[]{:S(2)}) collective-permute-start(bf16[96,2048]{1,0:T(8,128)(2,1)S(1)} %pad_maximum_fusion.2.refs_4_), channel_id=1, source_target_pairs={{0,48},{1,49},{16,0},{17,1},{32,16},{33,17},{48,32},{49,33},{2,50}... | collective-permute-start | bytes 1179656 | tf_op jit(solution)/shard_map/ppermute | solution.py:31
  63.8 13.5 %collective-permute-start.27 = (bf16[96,2048]{1,0:T(8,128)(2,1)S(1)}, bf16[96,2048]{1,0:T(8,128)(2,1)}, u32[]{:S(2)}, u32[]{:S(2)}) collective-permute-start(bf16[96,2048]{1,0:T(8,128)(2,1)S(1)} %pad_maximum_fusion.2.refs_4_), channel_id=1, source_target_pairs={{0,16},{1,17},{16,32},{17,33},{32,48},{33,49},{48,0},{49,1},{2,18}... | collective-permute-start | bytes 1179656 | tf_op jit(solution)/shard_map/ppermute | solution.py:31
  64.1 23.4 %collective-permute-start.11 = (bf16[96,2048]{1,0:T(8,128)(2,1)S(1)}, bf16[96,2048]{1,0:T(8,128)(2,1)}, u32[]{:S(2)}, u32[]{:S(2)}) collective-permute-start(bf16[96,2048]{1,0:T(8,128)(2,1)S(1)} %pad_maximum_fusion.1.refs_3_), channel_id=1, source_target_pairs={{0,16},{1,17},{16,32},{17,33},{32,48},{33,49},{48,0},{49,1},{2,18}... | collective-permute-start | bytes 1179656 | tf_op jit(solution)/shard_map/ppermute | solution.py:31
  64.2 23.3 %collective-permute-start.25 = (bf16[96,2048]{1,0:T(8,128)(2,1)S(1)}, bf16[96,2048]{1,0:T(8,128)(2,1)}, u32[]{:S(2)}, u32[]{:S(2)}) collective-permute-start(bf16[96,2048]{1,0:T(8,128)(2,1)S(1)} %pad_maximum_fusion.1.refs_3_), channel_id=1, source_target_pairs={{0,48},{1,49},{16,0},{17,1},{32,16},{33,17},{48,32},{49,33},{2,50}... | collective-permute-start | bytes 1179656 | tf_op jit(solution)/shard_map/ppermute | solution.py:31
  74.0 33.8 %collective-permute-start.22 = (bf16[4,16,4096]{2,1,0:T(8,128)(2,1)S(1)}, bf16[4,16,4096]{2,1,0:T(8,128)(2,1)S(1)}, u32[]{:S(2)}, u32[]{:S(2)}) collective-permute-start(bf16[4,16,4096]{2,1,0:T(8,128)(2,1)S(1)} %pad_maximum_fusion.refs_5_.refs_13_.refs_21_.refs_29_), channel_id=1, source_target_pairs={{0,4},{1,5},{16,20},{17,21},{32,36},{33,37},{48,52},{49,53},{2,6},... | collective-permute-start | bytes 1572872 | tf_op jit(solution)/shard_map/ppermute | solution.py:31
  77.3 30.6 %collective-permute-start.8 = (bf16[64,2048]{1,0:T(8,128)(2,1)S(1)}, bf16[64,2048]{1,0:T(8,128)(2,1)S(1)}, u32[]{:S(2)}, u32[]{:S(2)}) collective-permute-start(bf16[64,2048]{1,0:T(8,128)(2,1)S(1)} %add_add_fusion.refs_2_), channel_id=1, source_target_pairs={{0,32},{1,33},{16,48},{17,49},{32,0},{33,1},{48,16},{49,17},{2,34}... | collective-permute-start | bytes 786440 | tf_op jit(solution)/shard_map/ppermute | solution.py:31
  87.5 33.8 %collective-permute-start.19 = (bf16[4,16,4096]{2,1,0:T(8,128)(2,1)S(1)}, bf16[4,16,4096]{2,1,0:T(8,128)(2,1)S(1)}, u32[]{:S(2)}, u32[]{:S(2)}) collective-permute-start(bf16[4,16,4096]{2,1,0:T(8,128)(2,1)S(1)} %collective-permute-done.17.refs_6_.refs_14_.refs_22_.refs_30_), channel_id=1, source_target_pairs={{0,12},{1,13},{16,28},{17,29},{32,44},{33,45},{48,60},{49,61},{2,1... | collective-permute-start | bytes 1572872 | tf_op jit(solution)/shard_map/ppermute | solution.py:31
  87.5 33.8 %collective-permute-start.23 = (bf16[4,16,4096]{2,1,0:T(8,128)(2,1)S(1)}, bf16[4,16,4096]{2,1,0:T(8,128)(2,1)S(1)}, u32[]{:S(2)}, u32[]{:S(2)}) collective-permute-start(bf16[4,16,4096]{2,1,0:T(8,128)(2,1)S(1)} %collective-permute-done.17.refs_6_.refs_14_.refs_22_.refs_30_), channel_id=1, source_target_pairs={{0,4},{1,5},{16,20},{17,21},{32,36},{33,37},{48,52},{49,53},{2,6},... | collective-permute-start | bytes 1572872 | tf_op jit(solution)/shard_map/ppermute | solution.py:31
  90.3 30.9 %collective-permute-start.21 = (bf16[4,16,4096]{2,1,0:T(8,128)(2,1)S(1)}, bf16[4,16,4096]{2,1,0:T(8,128)(2,1)S(1)}, u32[]{:S(2)}, u32[]{:S(2)}) collective-permute-start(bf16[4,16,4096]{2,1,0:T(8,128)(2,1)S(1)} %collective-permute-done.20.refs_9_.refs_17_.refs_25_.refs_33_), channel_id=1, source_target_pairs={{0,2},{1,3},{16,18},{17,19},{32,34},{33,35},{48,50},{49,51},{2,0},... | collective-permute-start | bytes 1572872 | tf_op jit(solution)/shard_map/ppermute | solution.py:31
  107.8 13.4 %collective-permute-start.15 = (bf16[96,2048]{1,0:T(8,128)(2,1)S(1)}, bf16[96,2048]{1,0:T(8,128)(2,1)S(1)}, u32[]{:S(2)}, u32[]{:S(2)}) collective-permute-start(bf16[96,2048]{1,0:T(8,128)(2,1)S(1)} %collective-permute-done.14.refs_4_), channel_id=1, source_target_pairs={{0,48},{1,49},{16,0},{17,1},{32,16},{33,17},{48,32},{49,33},{2,50}... | collective-permute-start | bytes 1179656 | tf_op jit(solution)/shard_map/ppermute | solution.py:31
  107.9 13.4 %collective-permute-start.12 = (bf16[96,2048]{1,0:T(8,128)(2,1)}, bf16[96,2048]{1,0:T(8,128)(2,1)S(1)}, u32[]{:S(2)}, u32[]{:S(2)}) collective-permute-start(bf16[96,2048]{1,0:T(8,128)(2,1)} %collective-permute-done.11.refs_6_), channel_id=1, source_target_pairs={{0,16},{1,17},{16,32},{17,33},{32,48},{33,49},{48,0},{49,1},{2,18}... | collective-permute-start | bytes 1179656 | tf_op jit(solution)/shard_map/ppermute | solution.py:31
  140.3 11.1 %all-to-all-start = ((f32[8,16,128]{2,1,0:T(8,128)}), f32[8,16,128]{2,1,0:T(8,128)S(1)}, u32[]{:S(2)}, u32[]{:S(2)}) async-start(f32[8,16,128]{2,1,0:T(8,128)} %slice_add_fusion), calls=%async_computation | async-start | bytes 131072 | tf_op jit(solution)/shard_map/all_to_all | solution.py:223
  (11 other events, 37.6 us)
where the time goes:
time: 153 us; the launch traced here: 152 us
  waiting for transfers between devices  55.7 us (36%)
  Pallas kernels  42.6 us (28%)
  starting transfers between devices  40.6 us (27%)
  local copies, waits for them, and re-layouts  10.9 us (7%)
  other arithmetic  2.03 us (1%)
    ppermute x29, waiting for transfers between devices, moved(): return lax.ppermute(value, AXES, pairs)  47.9 us
    pallas_call x3, Pallas kernels, contracted(): pl.pallas_call(functools.partial(kernel, [len(window[j]) for j in js], le...  42.6 us
    ppermute x29, starting transfers between devices, moved(): return lax.ppermute(value, AXES, pairs)  37.2 us
    all_to_all x1, waiting for transfers between devices, per_device(): blocks = lax.all_to_all(own, 'grp', 0, 0, tiled=True)  7.76 us
    unnamed x11, local copies, waits for them, and re-layouts  4.63 us
    all_to_all x1, starting transfers between devices, per_device(): blocks = lax.all_to_all(own, 'grp', 0, 0, tiled=True)  3.35 us
  transfers between devices with their start and end apart: 30, of which 10 were waited for; matrix products, arithmetic and copies ran while one was open for 5% of the time, Pallas kernels for 17%

commit v1 on v0

--- a/solution.py
+++ b/solution.py
@@ -10,7 +10,7 @@
 
 AXES = ("grp", "pair")
 DT = 16
-VMEM_MIB = 48
+VMEM_MIB = 42
 
 
 def linear(x, y, z, c):
@@ -120,29 +120,29 @@
         for lane in range(2 * blocks):
             tile[h, lane] = product[:, 128 * lane : 128 * (lane + 1)]
 
-    def regrouped(n, q, h, a):
+    def regrouped(n, h, a):
         lane, at = 2 * n + a // 2, (a % 2) * 64
         parts = [
-            tile[h, lane, pl.ds(4 * q + d, 32, stride=DT), :][:, at : at + 64].astype(jnp.bfloat16)
-            for d in range(4)
+            tile[h, lane, pl.ds(d, 32, stride=DT), :][:, at : at + 64].astype(jnp.bfloat16)
+            for d in range(DT)
         ]
         return jnp.concatenate(parts, axis=1)
 
-    for q in range(DT // 4):
-        lefts = []
+    lefts = []
+    for n in range(blocks):
+        group = [regrouped(n, h, a) for h in range(2) for a in range(4)]
+        lefts.append(jnp.concatenate(group, axis=0))
+    if emit:
         for n in range(blocks):
-            group = [regrouped(n, q, h, a) for h in range(2) for a in range(4)]
-            lefts.append(jnp.concatenate(group, axis=0))
-        if emit:
-            for n in range(blocks):
-                o_ref[n, q] = lefts[n]
-            continue
-        lefts += [s_ref[0, q] for s_ref in s_refs]
+            o_ref[n] = lefts[n]
+    else:
+        lefts = [s_ref[0] for s_ref in s_refs] + lefts
+        partial = None
         for n in range(total_blocks):
-            amp = jnp.concatenate(
-                [t_refs[8 * n + r][0, :, 256 * q : 256 * (q + 1)] for r in range(8)], axis=0
-            )
-            total[...] += lax.dot_general(amp, lefts[n], NT, preferred_element_type=jnp.float32)
+            amp = jnp.concatenate([t_refs[8 * n + r][0] for r in range(8)], axis=0)
+            term = lax.dot_general(amp, lefts[n], NT, preferred_element_type=jnp.float32)
+            partial = term if partial is None else partial + term
+        total[...] += partial
 
     if emit:
         return
@@ -150,10 +150,11 @@
     @pl.when(step == pl.num_programs(0) - 1)
     def _():
         if last:
-            x, low, k = pos_ref[0], pos_ref[1], pos_ref[2]
+            x, low, k, high, z = [pos_ref[i] for i in range(5)]
             for dx in range(4):
                 for dy in range(2):
                     to = lax.rem(x + dx, 4) * 2 + (low + dy) % 2
+                    to = lax.rem(to // 4 + high, 2) * 4 + lax.rem(to % 4 - z + 4, 4)
                     for e in range(2):
                         row = (dx * 2 + dy) * 16 + e * 8
                         o_ref[to, (k + e) % 2] = total[row : row + 8, :]
@@ -171,18 +172,18 @@
         in_specs += [full(piece.shape) for piece in window[j]]
         operands += window[j]
     if not emit:
-        for j in [*js, *(j for j, _, _ in stored)]:
+        for j in [*(j for j, _, _ in stored), *js]:
             in_specs += [pl.BlockSpec((1, 16, DT * 64), lambda i, pos, j=j: (j, 0, i))] * 8
             operands += amps
     for _, left, n in stored:
-        in_specs.append(pl.BlockSpec((1, DT // 4, 256, 256), lambda i, pos, n=n: (n, i, 0, 0)))
+        in_specs.append(pl.BlockSpec((1, 256, DT * 64), lambda i, pos, n=n: (n, 0, i)))
         operands.append(left)
     if acc is not None:
         in_specs.append(full((128, 256)))
         operands.append(acc)
     if emit:
-        out = jax.ShapeDtypeStruct((blocks, n_d // 4, 256, 256), jnp.bfloat16)
-        out_specs = pl.BlockSpec((blocks, DT // 4, 256, 256), lambda i, pos: (0, i, 0, 0))
+        out = jax.ShapeDtypeStruct((blocks, 256, n_d * 64), jnp.bfloat16)
+        out_specs = pl.BlockSpec((blocks, 256, DT * 64), lambda i, pos: (0, 0, i))
     else:
         out = jax.ShapeDtypeStruct((8, 2, 8, 256) if last else (128, 256), jnp.float32)
         out_specs = full(out.shape)
@@ -209,7 +210,7 @@
 
 def per_device(amplitudes, cholesky):
     x, y, z, k = position()
-    pos = jnp.stack([x, y % 2, k]).astype(jnp.int32)
+    pos = jnp.stack([x, y % 2, k, y // 2, z]).astype(jnp.int32)
     swap = lambda x, y, z, c: (x, y, z, 1 - c)
     chol = (cholesky, moved(cholesky, swap))
     window = gathered_window(cholesky, x, y, k)
@@ -220,8 +221,11 @@
     acc = contracted(pos, chol, window, amps, (2,), stored=stored, last=True)
     parts = acc.reshape(8, 16, 256)
     own = parts[:, :, :128] + moved(parts[:, :, 128:], swap)
-    blocks = lax.all_to_all(own, "grp", 0, 0, tiled=True)
-    result = jnp.sum(blocks, axis=0).reshape(16, 4, 32)
+    half = own[:4] + moved(own[4:], lambda x, y, z, c: (x, y + 2, z, c))
+    result = half[0]
+    for j in (2, 1, 3):
+        result = result + moved(half[j], lambda x, y, z, c: (x, y, z + j, c))
+    result = result.reshape(16, 4, 32)
     result = lax.dynamic_slice_in_dim(jnp.concatenate([result, result], axis=1), (4 - x) % 4, 4, 1)
     return result.transpose(2, 1, 0)
 

time: 153 us -> 150 us (0.980)
  Pallas kernels: 42.6 us -> 37.4 us
  local copies, waits for them, and re-layouts: 10.9 us -> 13.1 us
    ppermute x29 -> x33, waiting for transfers between devices: 47.9 us -> 55.8 us  [moved(): return lax.ppermute(value, AXES, pairs)]
    all_to_all x1 -> x0, waiting for transfers between devices: 7.76 us -> none  [per_device(): blocks = lax.all_to_all(own, 'grp', 0, 0, tiled=True)]
    pallas_call x3, Pallas kernels: 42.6 us -> 37.4 us  [contracted(): pl.pallas_call(functools.partial(kernel, [len(window[j]) for j in js], le...]
    ppermute x29 -> x33, starting transfers between devices: 37.2 us -> 40.8 us  [moved(): return lax.ppermute(value, AXES, pairs)]
    all_to_all x1 -> x0, starting transfers between devices: 3.35 us -> none  [per_device(): blocks = lax.all_to_all(own, 'grp', 0, 0, tiled=True)]
    unnamed x11, local copies, waits for them, and re-layouts: 4.63 us -> 6.74 us
  transfers between devices with their start and end apart: 30 -> 33, of which waited for: 10 -> 12; matrix products, arithmetic and copies ran while one was open for 5% -> 5% of each run, Pallas kernels for 17% -> 16%
where the time goes in v1:
time: 150 us; the launch traced here: 149 us
  waiting for transfers between devices  55.8 us (37%)
  starting transfers between devices  40.8 us (27%)
  Pallas kernels  37.4 us (25%)
  local copies, waits for them, and re-layouts  13.1 us (9%)
    ppermute x33, waiting for transfers between devices, moved(): return lax.ppermute(value, AXES, pairs)  55.8 us
    ppermute x33, starting transfers between devices, moved(): return lax.ppermute(value, AXES, pairs)  40.8 us
    pallas_call x3, Pallas kernels, contracted(): pl.pallas_call(functools.partial(kernel, [len(window[j]) for j in js], le...  37.4 us
    unnamed x11, local copies, waits for them, and re-layouts  6.74 us
    reshape x2, local copies, waits for them, and re-layouts, gathered_amplitudes(): amplitudes.reshape(n_ij, n_d, 2, 4, 64).transpose(2, 3, 0, 1, 4)  3 us
  transfers between devices with their start and end apart: 33, of which 12 were waited for; matrix products, arithmetic and copies ran while one was open for 5% of the time, Pallas kernels for 16%

profile of v1, /device:TPU:0, one launch (start us, length us, event | category | flops | bytes accessed | tf_op | source)
XLA Modules:
  0.0 148.8 jit_solution(12378916887629679673)
XLA Ops:
  0.0 2.2 %slice_bitcast_fusion.2 = (bf16[64,2048]{1,0:T(8,128)(2,1)}, bf16[64,2048]{1,0:T(8,128)(2,1)}, bf16[64,2048]{1,0:T(8,128)(2,1)}, bf16[64,2048]{1,0:T(8,128)(2,1)}) fusion(bf16[32,64,2048]{2,1,0:T(8,128)(2,1)} %refs_0_.5), kind=kLoop, calls=%fused_computation.9 | loop fusion | bytes 2097152 | tf_op jit(solution)/shard_map/squeeze | solution.py:42
  2.2 3.5 %collective-permute-start.1 = (bf16[64,2048]{1,0:T(8,128)(2,1)}, bf16[64,2048]{1,0:T(8,128)(2,1)S(1)}, u32[]{:S(2)}, u32[]{:S(2)}) collective-permute-start(bf16[64,2048]{1,0:T(8,128)(2,1)} %get-tuple-element.5), channel_id=1, source_target_pairs={{0,4},{16,20},{32,36},{48,52},{64,69},{80,85},{96,101},{112,117}} | collective-permute-start | bytes 786440 | tf_op jit(solution)/shard_map/ppermute | solution.py:31
  5.7 1.9 %collective-permute-start.2 = (bf16[64,2048]{1,0:T(8,128)(2,1)}, bf16[64,2048]{1,0:T(8,128)(2,1)S(1)}, u32[]{:S(2)}, u32[]{:S(2)}) collective-permute-start(bf16[64,2048]{1,0:T(8,128)(2,1)} %get-tuple-element.7), channel_id=1, source_target_pairs={{0,12},{16,28},{32,44},{48,60},{64,77},{80,93},{96,109},{112,125}} | collective-permute-start | bytes 786440 | tf_op jit(solution)/shard_map/ppermute | solution.py:31
  10.3 2.2 %reshape.12 = bf16[8,64,2,4,64]{4,3,2,1,0:T(4,128)(2,1)S(1)} reshape(bf16[8,64,512]{2,1,0:T(8,128)(2,1)} %param.2) | data formatting | bytes 1048576 | tf_op jit(solution)/shard_map/reshape | solution.py:75
  17.5 4.6 %collective-permute-start.7 = (bf16[64,2048]{1,0:T(8,128)(2,1)S(1)}, bf16[64,2048]{1,0:T(8,128)(2,1)S(1)}, u32[]{:S(2)}, u32[]{:S(2)}) collective-permute-start(bf16[64,2048]{1,0:T(8,128)(2,1)S(1)} %add_add_fusion.1), channel_id=1, source_target_pairs={{0,64},{16,80},{32,96},{48,112},{65,1},{81,17},{97,33},{113,49},{4... | collective-permute-start | bytes 786440 | tf_op jit(solution)/shard_map/ppermute | solution.py:31
  22.3 3.7 %collective-permute-done.7 = bf16[64,2048]{1,0:T(8,128)(2,1)S(1)} collective-permute-done((bf16[64,2048]{1,0:T(8,128)(2,1)S(1)}, bf16[64,2048]{1,0:T(8,128)(2,1)S(1)}, u32[]{:S(2)}, u32[]{:S(2)}) %collective-permute-start.7) | collective-permute-done | bytes 262176 | tf_op jit(solution)/shard_map/ppermute | solution.py:31
  26.3 3.2 %collective-permute-start.9 = (bf16[64,2048]{1,0:T(8,128)(2,1)S(1)}, bf16[64,2048]{1,0:T(8,128)(2,1)S(1)}, u32[]{:S(2)}, u32[]{:S(2)}) collective-permute-start(bf16[64,2048]{1,0:T(8,128)(2,1)S(1)} %add_add_fusion.refs_2_), channel_id=1, source_target_pairs={{0,12},{1,13},{16,28},{17,29},{32,44},{33,45},{48,60},{49,61},{2,1... | collective-permute-start | bytes 786440 | tf_op jit(solution)/shard_map/ppermute | solution.py:31
  29.6 7.2 %collective-permute-done.10 = bf16[64,2048]{1,0:T(8,128)(2,1)S(1)} collective-permute-done((bf16[64,2048]{1,0:T(8,128)(2,1)S(1)}, bf16[64,2048]{1,0:T(8,128)(2,1)S(1)}, u32[]{:S(2)}, u32[]{:S(2)}) %collective-permute-start.10) | collective-permute-done | bytes 262176 | tf_op jit(solution)/shard_map/ppermute | solution.py:31
  36.8 5.3 %collective-permute-done.13 = bf16[64,2048]{1,0:T(8,128)(2,1)S(1)} collective-permute-done((bf16[64,2048]{1,0:T(8,128)(2,1)S(1)}, bf16[64,2048]{1,0:T(8,128)(2,1)S(1)}, u32[]{:S(2)}, u32[]{:S(2)}) %collective-permute-start.13) | collective-permute-done | bytes 262176 | tf_op jit(solution)/shard_map/ppermute | solution.py:31
  43.0 4.0 %collective-permute-start.24 = (bf16[64,2048]{1,0:T(8,128)(2,1)S(1)}, bf16[64,2048]{1,0:T(8,128)(2,1)S(1)}, u32[]{:S(2)}, u32[]{:S(2)}) collective-permute-start(bf16[64,2048]{1,0:T(8,128)(2,1)S(1)} %add_add_fusion.refs_2_), channel_id=1, source_target_pairs={{0,48},{1,49},{16,0},{17,1},{32,16},{33,17},{48,32},{49,33},{2,50}... | collective-permute-start | bytes 786440 | tf_op jit(solution)/shard_map/ppermute | solution.py:31
  47.1 5.0 %collective-permute-done.24.refs_2_ = bf16[64,2048]{1,0:T(8,128)(2,1)S(1)} collective-permute-done((bf16[64,2048]{1,0:T(8,128)(2,1)S(1)}, bf16[64,2048]{1,0:T(8,128)(2,1)S(1)}, u32[]{:S(2)}, u32[]{:S(2)}) %collective-permute-start.24) | collective-permute-done | bytes 262176 | tf_op jit(solution)/shard_map/ppermute | solution.py:31
  53.4 8.0 %collective-permute-done.26.refs_5_ = bf16[64,2048]{1,0:T(8,128)(2,1)S(1)} collective-permute-done((bf16[64,2048]{1,0:T(8,128)(2,1)S(1)}, bf16[64,2048]{1,0:T(8,128)(2,1)S(1)}, u32[]{:S(2)}, u32[]{:S(2)}) %collective-permute-start.26) | collective-permute-done | bytes 262176 | tf_op jit(solution)/shard_map/ppermute | solution.py:31
  64.2 3.2 %collective-permute-start.25 = (bf16[96,2048]{1,0:T(8,128)(2,1)S(1)}, bf16[96,2048]{1,0:T(8,128)(2,1)}, u32[]{:S(2)}, u32[]{:S(2)}) collective-permute-start(bf16[96,2048]{1,0:T(8,128)(2,1)S(1)} %pad_maximum_fusion.1.refs_3_), channel_id=1, source_target_pairs={{0,48},{1,49},{16,0},{17,1},{32,16},{33,17},{48,32},{49,33},{2,50}... | collective-permute-start | bytes 1179656 | tf_op jit(solution)/shard_map/ppermute | solution.py:31
  67.4 6.6 %collective-permute-done.14.refs_4_ = bf16[96,2048]{1,0:T(8,128)(2,1)S(1)} collective-permute-done((bf16[96,2048]{1,0:T(8,128)(2,1)S(1)}, bf16[96,2048]{1,0:T(8,128)(2,1)S(1)}, u32[]{:S(2)}, u32[]{:S(2)}) %collective-permute-start.14) | collective-permute-done | bytes 393248 | tf_op jit(solution)/shard_map/ppermute | solution.py:31
  74.0 2.3 %collective-permute-start.22 = (bf16[4,16,4096]{2,1,0:T(8,128)(2,1)S(1)}, bf16[4,16,4096]{2,1,0:T(8,128)(2,1)S(1)}, u32[]{:S(2)}, u32[]{:S(2)}) collective-permute-start(bf16[4,16,4096]{2,1,0:T(8,128)(2,1)S(1)} %pad_maximum_fusion.refs_5_.refs_13_.refs_21_.refs_29_), channel_id=1, source_target_pairs={{0,4},{1,5},{16,20},{17,21},{32,36},{33,37},{48,52},{49,53},{2,6},... | collective-permute-start | bytes 1572872 | tf_op jit(solution)/shard_map/ppermute | solution.py:31
  77.5 9.9 %collective-permute-done.11.refs_6_ = bf16[96,2048]{1,0:T(8,128)(2,1)} collective-permute-done((bf16[96,2048]{1,0:T(8,128)(2,1)S(1)}, bf16[96,2048]{1,0:T(8,128)(2,1)}, u32[]{:S(2)}, u32[]{:S(2)}) %collective-permute-start.11) | collective-permute-done | bytes 393248 | tf_op jit(solution)/shard_map/ppermute | solution.py:31
  87.5 2.9 %collective-permute-start.23 = (bf16[4,16,4096]{2,1,0:T(8,128)(2,1)S(1)}, bf16[4,16,4096]{2,1,0:T(8,128)(2,1)S(1)}, u32[]{:S(2)}, u32[]{:S(2)}) collective-permute-start(bf16[4,16,4096]{2,1,0:T(8,128)(2,1)S(1)} %collective-permute-done.17.refs_6_.refs_14_.refs_22_.refs_30_), channel_id=1, source_target_pairs={{0,4},{1,5},{16,20},{17,21},{32,36},{33,37},{48,52},{49,53},{2,6},... | collective-permute-start | bytes 1572872 | tf_op jit(solution)/shard_map/ppermute | solution.py:31
  92.3 14.7 %shard_map.29.refs_38_.refs_39_ = bf16[2,256,4096]{2,1,0:T(8,128)(2,1)S(1)} custom-call(s32[5]{0:T(128)S(1)} %stack.23.pos_ref, bf16[32,64,2048]{2,1,0:T(8,128)(2,1)} %refs_0_.5, bf16[32,64,2048]{2,1,0:T(8,128)(2,1)} %collective-permute-done.refs_1_, bf16[64,2048]{1,0:T(8,128)(2,1)S(1)} %copy-done.2, bf16[96,2048]{1,0:T(8,128)(2,1)} %collective-permute-done.25.refs_3_, ...), custom_call_target="tpu_custom_call" | custom-call | flops 8589934592 | bytes 20971520 | tf_op jit(solution)/shard_map/pallas_call | solution.py:190
  107.1 2.0 %collective-permute-start.12 = (bf16[96,2048]{1,0:T(8,128)(2,1)}, bf16[96,2048]{1,0:T(8,128)(2,1)S(1)}, u32[]{:S(2)}, u32[]{:S(2)}) collective-permute-start(bf16[96,2048]{1,0:T(8,128)(2,1)} %collective-permute-done.11.refs_6_), channel_id=1, source_target_pairs={{0,16},{1,17},{16,32},{17,33},{32,48},{33,49},{48,0},{49,1},{2,18}... | collective-permute-start | bytes 1179656 | tf_op jit(solution)/shard_map/ppermute | solution.py:31
  109.1 3.4 %copy-done = bf16[32,64,2048]{2,1,0:T(8,128)(2,1)S(1)} copy-done((bf16[32,64,2048]{2,1,0:T(8,128)(2,1)S(1)}, bf16[32,64,2048]{2,1,0:T(8,128)(2,1)}, u32[]{:S(2)}) %copy-start) | copy-done | bytes 8388632
  112.5 9.1 %shard_map.28.refs_37_ = bf16[1,256,4096]{2,1,0:T(8,128)(2,1)S(1)} custom-call(s32[5]{0:T(128)S(1)} %stack.23.pos_ref, bf16[32,64,2048]{2,1,0:T(8,128)(2,1)S(1)} %copy-done, bf16[32,64,2048]{2,1,0:T(8,128)(2,1)} %collective-permute-done.refs_1_, bf16[64,2048]{1,0:T(8,128)(2,1)S(1)} %add_add_fusion.refs_2_, bf16[96,2048]{1,0:T(8,128)(2,1)S(1)} %pad_maximum_fusion.1.refs_3_, ...), custom_call_target="tpu_custom_call" | custom-call | flops 4294967296 | bytes 20971520 | tf_op jit(solution)/shard_map/pallas_call | solution.py:190
  121.6 13.6 %shard_map.30 = f32[8,2,8,256]{3,2,1,0:T(8,128)S(1)} custom-call(s32[5]{0:T(128)S(1)} %stack.23.pos_ref, bf16[32,64,2048]{2,1,0:T(8,128)(2,1)} %refs_0_.5, bf16[32,64,2048]{2,1,0:T(8,128)(2,1)} %collective-permute-done.refs_1_, bf16[64,2048]{1,0:T(8,128)(2,1)S(1)} %collective-permute-done.8.refs_2_, bf16[96,2048]{1,0:T(8,128)(2,1)S(1)} %collective-permute-done.12.refs_3_, ...), custom_call_target="tpu_custom_call" | custom-call | flops 4294967296 | bytes 20971520 | tf_op jit(solution)/shard_map/pallas_call | solution.py:190
  136.7 5.4 %collective-permute-done.29 = f32[4,16,128]{2,1,0:T(8,128)S(1)} collective-permute-done((f32[4,16,128]{2,1,0:T(8,128)S(1)}, f32[4,16,128]{2,1,0:T(8,128)S(1)}, u32[]{:S(2)}, u32[]{:S(2)}) %collective-permute-start.29) | collective-permute-done | bytes 32800 | tf_op jit(solution)/shard_map/ppermute | solution.py:31
  142.2 2.2 %collective-permute-start.31 = (f32[16,128]{1,0:T(8,128)S(1)}, f32[16,128]{1,0:T(8,128)S(1)}, u32[]{:S(2)}, u32[]{:S(2)}) collective-permute-start(f32[16,128]{1,0:T(8,128)S(1)} %get-tuple-element.15), channel_id=1, source_target_pairs={{0,16},{1,17},{16,32},{17,33},{32,48},{33,49},{48,0},{49,1},{2,18}... | collective-permute-start | bytes 24584 | tf_op jit(solution)/shard_map/ppermute | solution.py:31
  (78 shorter events, 22.3 us)
Async XLA Ops:
  0.0 90.3 %collective-permute-start = (bf16[32,64,2048]{2,1,0:T(8,128)(2,1)}, bf16[32,64,2048]{2,1,0:T(8,128)(2,1)}, u32[]{:S(2)}, u32[]{:S(2)}) collective-permute-start(bf16[32,64,2048]{2,1,0:T(8,128)(2,1)} %refs_0_.5), channel_id=1, source_target_pairs={{0,1},{1,0},{16,17},{17,16},{32,33},{33,32},{48,49},{49,48},{2,3},... | collective-permute-start | bytes 25165832 | tf_op jit(solution)/shard_map/ppermute | solution.py:31
  2.2 11.5 %collective-permute-start.1 = (bf16[64,2048]{1,0:T(8,128)(2,1)}, bf16[64,2048]{1,0:T(8,128)(2,1)S(1)}, u32[]{:S(2)}, u32[]{:S(2)}) collective-permute-start(bf16[64,2048]{1,0:T(8,128)(2,1)} %get-tuple-element.5), channel_id=1, source_target_pairs={{0,4},{16,20},{32,36},{48,52},{64,69},{80,85},{96,101},{112,117}} | collective-permute-start | bytes 786440 | tf_op jit(solution)/shard_map/ppermute | solution.py:31
  5.7 8.0 %collective-permute-start.2 = (bf16[64,2048]{1,0:T(8,128)(2,1)}, bf16[64,2048]{1,0:T(8,128)(2,1)S(1)}, u32[]{:S(2)}, u32[]{:S(2)}) collective-permute-start(bf16[64,2048]{1,0:T(8,128)(2,1)} %get-tuple-element.7), channel_id=1, source_target_pairs={{0,12},{16,28},{32,44},{48,60},{64,77},{80,93},{96,109},{112,125}} | collective-permute-start | bytes 786440 | tf_op jit(solution)/shard_map/ppermute | solution.py:31
  14.9 7.4 %collective-permute-start.5 = (bf16[64,2048]{1,0:T(8,128)(2,1)S(1)}, bf16[64,2048]{1,0:T(8,128)(2,1)S(1)}, u32[]{:S(2)}, u32[]{:S(2)}) collective-permute-start(bf16[64,2048]{1,0:T(8,128)(2,1)S(1)} %add_add_fusion.1), channel_id=1, source_target_pairs={{0,2},{16,18},{32,34},{48,50},{65,67},{81,83},{97,99},{113,115},{4... | collective-permute-start | bytes 786440 | tf_op jit(solution)/shard_map/ppermute | solution.py:31
  17.5 8.5 %collective-permute-start.7 = (bf16[64,2048]{1,0:T(8,128)(2,1)S(1)}, bf16[64,2048]{1,0:T(8,128)(2,1)S(1)}, u32[]{:S(2)}, u32[]{:S(2)}) collective-permute-start(bf16[64,2048]{1,0:T(8,128)(2,1)S(1)} %add_add_fusion.1), channel_id=1, source_target_pairs={{0,64},{16,80},{32,96},{48,112},{65,1},{81,17},{97,33},{113,49},{4... | collective-permute-start | bytes 786440 | tf_op jit(solution)/shard_map/ppermute | solution.py:31
  26.0 10.8 %collective-permute-start.10 = (bf16[64,2048]{1,0:T(8,128)(2,1)S(1)}, bf16[64,2048]{1,0:T(8,128)(2,1)S(1)}, u32[]{:S(2)}, u32[]{:S(2)}) collective-permute-start(bf16[64,2048]{1,0:T(8,128)(2,1)S(1)} %add_add_fusion.refs_2_), channel_id=1, source_target_pairs={{0,8},{1,9},{16,24},{17,25},{32,40},{33,41},{48,56},{49,57},{2,10}... | collective-permute-start | bytes 786440 | tf_op jit(solution)/shard_map/ppermute | solution.py:31
  26.3 15.9 %collective-permute-start.13 = (bf16[64,2048]{1,0:T(8,128)(2,1)S(1)}, bf16[64,2048]{1,0:T(8,128)(2,1)S(1)}, u32[]{:S(2)}, u32[]{:S(2)}) collective-permute-start(bf16[64,2048]{1,0:T(8,128)(2,1)S(1)} %add_add_fusion.refs_2_), channel_id=1, source_target_pairs={{0,4},{1,5},{16,20},{17,21},{32,36},{33,37},{48,52},{49,53},{2,6},... | collective-permute-start | bytes 786440 | tf_op jit(solution)/shard_map/ppermute | solution.py:31
  26.3 16.8 %collective-permute-start.9 = (bf16[64,2048]{1,0:T(8,128)(2,1)S(1)}, bf16[64,2048]{1,0:T(8,128)(2,1)S(1)}, u32[]{:S(2)}, u32[]{:S(2)}) collective-permute-start(bf16[64,2048]{1,0:T(8,128)(2,1)S(1)} %add_add_fusion.refs_2_), channel_id=1, source_target_pairs={{0,12},{1,13},{16,28},{17,29},{32,44},{33,45},{48,60},{49,61},{2,1... | collective-permute-start | bytes 786440 | tf_op jit(solution)/shard_map/ppermute | solution.py:31
  29.5 34.3 %collective-permute-start.17 = (bf16[4,16,4096]{2,1,0:T(8,128)(2,1)S(1)}, bf16[4,16,4096]{2,1,0:T(8,128)(2,1)S(1)}, u32[]{:S(2)}, u32[]{:S(2)}) collective-permute-start(bf16[4,16,4096]{2,1,0:T(8,128)(2,1)S(1)} %pad_maximum_fusion.refs_5_.refs_13_.refs_21_.refs_29_), channel_id=1, source_target_pairs={{0,2},{1,3},{16,18},{17,19},{32,34},{33,35},{48,50},{49,51},{2,0},... | collective-permute-start | bytes 1572872 | tf_op jit(solution)/shard_map/ppermute | solution.py:31
  36.8 27.3 %collective-permute-start.20 = (bf16[4,16,4096]{2,1,0:T(8,128)(2,1)S(1)}, bf16[4,16,4096]{2,1,0:T(8,128)(2,1)S(1)}, u32[]{:S(2)}, u32[]{:S(2)}) collective-permute-start(bf16[4,16,4096]{2,1,0:T(8,128)(2,1)S(1)} %pad_maximum_fusion.refs_5_.refs_13_.refs_21_.refs_29_), channel_id=1, source_target_pairs={{0,8},{1,9},{16,24},{17,25},{32,40},{33,41},{48,56},{49,57},{2,10}... | collective-permute-start | bytes 1572872 | tf_op jit(solution)/shard_map/ppermute | solution.py:31
  42.2 22.0 %collective-permute-start.18 = (bf16[4,16,4096]{2,1,0:T(8,128)(2,1)S(1)}, bf16[4,16,4096]{2,1,0:T(8,128)(2,1)S(1)}, u32[]{:S(2)}, u32[]{:S(2)}) collective-permute-start(bf16[4,16,4096]{2,1,0:T(8,128)(2,1)S(1)} %pad_maximum_fusion.refs_5_.refs_13_.refs_21_.refs_29_), channel_id=1, source_target_pairs={{0,12},{1,13},{16,28},{17,29},{32,44},{33,45},{48,60},{49,61},{2,1... | collective-permute-start | bytes 1572872 | tf_op jit(solution)/shard_map/ppermute | solution.py:31
  43.0 9.0 %collective-permute-start.24 = (bf16[64,2048]{1,0:T(8,128)(2,1)S(1)}, bf16[64,2048]{1,0:T(8,128)(2,1)S(1)}, u32[]{:S(2)}, u32[]{:S(2)}) collective-permute-start(bf16[64,2048]{1,0:T(8,128)(2,1)S(1)} %add_add_fusion.refs_2_), channel_id=1, source_target_pairs={{0,48},{1,49},{16,0},{17,1},{32,16},{33,17},{48,32},{49,33},{2,50}... | collective-permute-start | bytes 786440 | tf_op jit(solution)/shard_map/ppermute | solution.py:31
  52.8 8.6 %collective-permute-start.26 = (bf16[64,2048]{1,0:T(8,128)(2,1)S(1)}, bf16[64,2048]{1,0:T(8,128)(2,1)S(1)}, u32[]{:S(2)}, u32[]{:S(2)}) collective-permute-start(bf16[64,2048]{1,0:T(8,128)(2,1)S(1)} %add_add_fusion.refs_2_), channel_id=1, source_target_pairs={{0,16},{1,17},{16,32},{17,33},{32,48},{33,49},{48,0},{49,1},{2,18}... | collective-permute-start | bytes 786440 | tf_op jit(solution)/shard_map/ppermute | solution.py:31
  62.1 12.0 %collective-permute-start.14 = (bf16[96,2048]{1,0:T(8,128)(2,1)S(1)}, bf16[96,2048]{1,0:T(8,128)(2,1)S(1)}, u32[]{:S(2)}, u32[]{:S(2)}) collective-permute-start(bf16[96,2048]{1,0:T(8,128)(2,1)S(1)} %pad_maximum_fusion.2.refs_4_), channel_id=1, source_target_pairs={{0,48},{1,49},{16,0},{17,1},{32,16},{33,17},{48,32},{49,33},{2,50}... | collective-permute-start | bytes 1179656 | tf_op jit(solution)/shard_map/ppermute | solution.py:31
  63.8 13.5 %collective-permute-start.27 = (bf16[96,2048]{1,0:T(8,128)(2,1)S(1)}, bf16[96,2048]{1,0:T(8,128)(2,1)}, u32[]{:S(2)}, u32[]{:S(2)}) collective-permute-start(bf16[96,2048]{1,0:T(8,128)(2,1)S(1)} %pad_maximum_fusion.2.refs_4_), channel_id=1, source_target_pairs={{0,16},{1,17},{16,32},{17,33},{32,48},{33,49},{48,0},{49,1},{2,18}... | collective-permute-start | bytes 1179656 | tf_op jit(solution)/shard_map/ppermute | solution.py:31
  64.1 23.4 %collective-permute-start.11 = (bf16[96,2048]{1,0:T(8,128)(2,1)S(1)}, bf16[96,2048]{1,0:T(8,128)(2,1)}, u32[]{:S(2)}, u32[]{:S(2)}) collective-permute-start(bf16[96,2048]{1,0:T(8,128)(2,1)S(1)} %pad_maximum_fusion.1.refs_3_), channel_id=1, source_target_pairs={{0,16},{1,17},{16,32},{17,33},{32,48},{33,49},{48,0},{49,1},{2,18}... | collective-permute-start | bytes 1179656 | tf_op jit(solution)/shard_map/ppermute | solution.py:31
  64.2 23.3 %collective-permute-start.25 = (bf16[96,2048]{1,0:T(8,128)(2,1)S(1)}, bf16[96,2048]{1,0:T(8,128)(2,1)}, u32[]{:S(2)}, u32[]{:S(2)}) collective-permute-start(bf16[96,2048]{1,0:T(8,128)(2,1)S(1)} %pad_maximum_fusion.1.refs_3_), channel_id=1, source_target_pairs={{0,48},{1,49},{16,0},{17,1},{32,16},{33,17},{48,32},{49,33},{2,50}... | collective-permute-start | bytes 1179656 | tf_op jit(solution)/shard_map/ppermute | solution.py:31
  74.0 32.9 %collective-permute-start.22 = (bf16[4,16,4096]{2,1,0:T(8,128)(2,1)S(1)}, bf16[4,16,4096]{2,1,0:T(8,128)(2,1)S(1)}, u32[]{:S(2)}, u32[]{:S(2)}) collective-permute-start(bf16[4,16,4096]{2,1,0:T(8,128)(2,1)S(1)} %pad_maximum_fusion.refs_5_.refs_13_.refs_21_.refs_29_), channel_id=1, source_target_pairs={{0,4},{1,5},{16,20},{17,21},{32,36},{33,37},{48,52},{49,53},{2,6},... | collective-permute-start | bytes 1572872 | tf_op jit(solution)/shard_map/ppermute | solution.py:31
  77.3 29.8 %collective-permute-start.8 = (bf16[64,2048]{1,0:T(8,128)(2,1)S(1)}, bf16[64,2048]{1,0:T(8,128)(2,1)S(1)}, u32[]{:S(2)}, u32[]{:S(2)}) collective-permute-start(bf16[64,2048]{1,0:T(8,128)(2,1)S(1)} %add_add_fusion.refs_2_), channel_id=1, source_target_pairs={{0,32},{1,33},{16,48},{17,49},{32,0},{33,1},{48,16},{49,17},{2,34}... | collective-permute-start | bytes 786440 | tf_op jit(solution)/shard_map/ppermute | solution.py:31
  87.5 34.1 %collective-permute-start.19 = (bf16[4,16,4096]{2,1,0:T(8,128)(2,1)S(1)}, bf16[4,16,4096]{2,1,0:T(8,128)(2,1)S(1)}, u32[]{:S(2)}, u32[]{:S(2)}) collective-permute-start(bf16[4,16,4096]{2,1,0:T(8,128)(2,1)S(1)} %collective-permute-done.17.refs_6_.refs_14_.refs_22_.refs_30_), channel_id=1, source_target_pairs={{0,12},{1,13},{16,28},{17,29},{32,44},{33,45},{48,60},{49,61},{2,1... | collective-permute-start | bytes 1572872 | tf_op jit(solution)/shard_map/ppermute | solution.py:31
  87.5 34.1 %collective-permute-start.23 = (bf16[4,16,4096]{2,1,0:T(8,128)(2,1)S(1)}, bf16[4,16,4096]{2,1,0:T(8,128)(2,1)S(1)}, u32[]{:S(2)}, u32[]{:S(2)}) collective-permute-start(bf16[4,16,4096]{2,1,0:T(8,128)(2,1)S(1)} %collective-permute-done.17.refs_6_.refs_14_.refs_22_.refs_30_), channel_id=1, source_target_pairs={{0,4},{1,5},{16,20},{17,21},{32,36},{33,37},{48,52},{49,53},{2,6},... | collective-permute-start | bytes 1572872 | tf_op jit(solution)/shard_map/ppermute | solution.py:31
  90.3 31.2 %collective-permute-start.21 = (bf16[4,16,4096]{2,1,0:T(8,128)(2,1)S(1)}, bf16[4,16,4096]{2,1,0:T(8,128)(2,1)S(1)}, u32[]{:S(2)}, u32[]{:S(2)}) collective-permute-start(bf16[4,16,4096]{2,1,0:T(8,128)(2,1)S(1)} %collective-permute-done.20.refs_9_.refs_17_.refs_25_.refs_33_), channel_id=1, source_target_pairs={{0,2},{1,3},{16,18},{17,19},{32,34},{33,35},{48,50},{49,51},{2,0},... | collective-permute-start | bytes 1572872 | tf_op jit(solution)/shard_map/ppermute | solution.py:31
  107.0 14.6 %collective-permute-start.15 = (bf16[96,2048]{1,0:T(8,128)(2,1)S(1)}, bf16[96,2048]{1,0:T(8,128)(2,1)S(1)}, u32[]{:S(2)}, u32[]{:S(2)}) collective-permute-start(bf16[96,2048]{1,0:T(8,128)(2,1)S(1)} %collective-permute-done.14.refs_4_), channel_id=1, source_target_pairs={{0,48},{1,49},{16,0},{17,1},{32,16},{33,17},{48,32},{49,33},{2,50}... | collective-permute-start | bytes 1179656 | tf_op jit(solution)/shard_map/ppermute | solution.py:31
  107.1 14.5 %collective-permute-start.12 = (bf16[96,2048]{1,0:T(8,128)(2,1)}, bf16[96,2048]{1,0:T(8,128)(2,1)S(1)}, u32[]{:S(2)}, u32[]{:S(2)}) collective-permute-start(bf16[96,2048]{1,0:T(8,128)(2,1)} %collective-permute-done.11.refs_6_), channel_id=1, source_target_pairs={{0,16},{1,17},{16,32},{17,33},{32,48},{33,49},{48,0},{49,1},{2,18}... | collective-permute-start | bytes 1179656 | tf_op jit(solution)/shard_map/ppermute | solution.py:31
  (14 other events, 51.9 us)

commit v2 on v1

--- a/solution.py
+++ b/solution.py
@@ -11,6 +11,7 @@
 AXES = ("grp", "pair")
 DT = 16
 VMEM_MIB = 42
+VMEM_FIRST = 50
 
 
 def linear(x, y, z, c):
@@ -36,7 +37,7 @@
     return p // 4, (g // 4) * 2 + (p // 2) % 2, g % 4, p % 2
 
 
-def gathered_window(cholesky, x, y, k):
+def gathered_window(cholesky, amplitudes, x, y, k):
     at_root = lambda x, y, c: x == 0 and y % 2 == 0 and c == 0
     got = [
         moved(cholesky[dx], lambda x, y, z, c: (dx, y, z, y // 2) if at_root(x, y, c) else None)
@@ -47,6 +48,7 @@
     )
     own = jnp.where((x == 0) & (y == 0) & (k == 0), cholesky[0], jnp.zeros_like(cholesky[0]))
     piece = own + got[0] + got[1] + got[2] + got[3]
+    piece, amplitudes = lax.optimization_barrier((piece, amplitudes))
     spread = [
         moved(piece, lambda x, y, z, c: (x, y + dy, z, c) if y == 2 * c else None)
         for dy in (1, 3, 2)
@@ -62,21 +64,52 @@
     up, down = moved(upper, rise), moved(lower, fall)
     up_more, down_more = moved(lower, rise), moved(upper, fall)
     up_far, down_far = moved(up, rise), moved(down, fall)
-    return [
+    window = [
         [piece, upper, lower],
         [early[0], down_more, down],
         [early[2], up_far, down_far],
         [early[1], up, up_more],
     ]
-
-
-def gathered_amplitudes(amplitudes, z, k):
-    n_ij, n_d = amplitudes.shape[:2]
-    parts = amplitudes.reshape(n_ij, n_d, 2, 4, 64).transpose(2, 3, 0, 1, 4).reshape(2, 4, n_ij, n_d * 64)
-    twice = jnp.concatenate([parts, parts], axis=1)
-    turned = lax.dynamic_slice_in_dim(twice, z, 4, 1)
-    mine = lax.dynamic_index_in_dim(turned, k, 0, keepdims=False)
-    other = lax.dynamic_index_in_dim(turned, 1 - k, 0, keepdims=False)
+    return window, amplitudes
+
+
+def relaid(pos, amplitudes):
+    n_ij, n_d, n_c = amplitudes.shape
+
+    def body(pos_ref, x_ref, o_ref, wide):
+        k, z = pos_ref[2], pos_ref[4]
+        for lane in range(n_c // 128):
+            wide[lane] = x_ref[:, :, 128 * lane : 128 * (lane + 1)].astype(jnp.float32).reshape(-1, 128)
+        for lane in range(n_c // 128):
+            half = lax.rem(lane // 2 + k, 2)
+            first = lax.rem(2 * (lane % 2) - z + 4, 4)
+            second = lax.rem(2 * (lane % 2) + 1 - z + 4, 4)
+            for d in range(0, n_d, 2):
+                even = wide[lane, pl.ds(d, n_ij, stride=n_d), :]
+                odd = wide[lane, pl.ds(d + 1, n_ij, stride=n_d), :]
+                left = jnp.concatenate([even[:, :64], odd[:, :64]], axis=1).astype(jnp.bfloat16)
+                right = jnp.concatenate([even[:, 64:], odd[:, 64:]], axis=1).astype(jnp.bfloat16)
+                o_ref[half, first, :, 64 * d : 64 * d + 128] = left
+                o_ref[half, second, :, 64 * d : 64 * d + 128] = right
+
+    out = (2, 4, n_ij, n_d * 64)
+    return pl.pallas_call(
+        body,
+        grid_spec=pltpu.PrefetchScalarGridSpec(
+            num_scalar_prefetch=1,
+            grid=(1,),
+            in_specs=[pl.BlockSpec(amplitudes.shape, lambda i, pos: (0, 0, 0))],
+            out_specs=pl.BlockSpec(out, lambda i, pos: (0, 0, 0, 0)),
+            scratch_shapes=[pltpu.VMEM((n_c // 128, n_ij * n_d, 128), jnp.float32)],
+        ),
+        out_shape=jax.ShapeDtypeStruct(out, jnp.bfloat16),
+        compiler_params=pltpu.CompilerParams(vmem_limit_bytes=8 * 1024 * 1024),
+        cost_estimate=pl.CostEstimate(flops=1000000, bytes_accessed=1024 * 1024, transcendentals=0),
+    )(pos, amplitudes)
+
+
+def gathered_amplitudes(pos, amplitudes):
+    mine, other = relaid(pos, amplitudes)
     came = moved(other, lambda x, y, z, c: (x, y, z, 1 - c))
     a0 = jnp.concatenate([mine, came], axis=1)
     across = lambda x, y, z, c: (x, y ^ 1, z, c)
@@ -201,7 +234,7 @@
             ],
         ),
         out_shape=out,
-        compiler_params=pltpu.CompilerParams(vmem_limit_bytes=VMEM_MIB * 1024 * 1024),
+        compiler_params=pltpu.CompilerParams(vmem_limit_bytes=(VMEM_FIRST if emit and blocks == 1 else VMEM_MIB) * 1024 * 1024),
         cost_estimate=pl.CostEstimate(
             flops=blocks * 2 * 4096 * 256 * 2048, bytes_accessed=20 * 1024 * 1024, transcendentals=0
         ),
@@ -213,8 +246,8 @@
     pos = jnp.stack([x, y % 2, k, y // 2, z]).astype(jnp.int32)
     swap = lambda x, y, z, c: (x, y, z, 1 - c)
     chol = (cholesky, moved(cholesky, swap))
-    window = gathered_window(cholesky, x, y, k)
-    amps = gathered_amplitudes(amplitudes, z, k)
+    window, amplitudes = gathered_window(cholesky, amplitudes, x, y, k)
+    amps = gathered_amplitudes(pos, amplitudes)
     first = contracted(pos, chol, window, amps, (0,), emit=True)
     second = contracted(pos, chol, window, amps, (1, 3), emit=True)
     stored = ((0, first, 0), (1, second, 0), (3, second, 1))

time: 150 us -> 135 us (0.900)
  waiting for transfers between devices: 55.8 us -> 44.2 us
  local copies, waits for them, and re-layouts: 13.1 us -> 3.15 us
  starting transfers between devices: 40.8 us -> 46 us
  Pallas kernels: 37.4 us -> 39.4 us
    ppermute x33, waiting for transfers between devices: 55.8 us -> 44.2 us  [moved(): return lax.ppermute(value, AXES, pairs)]
    unnamed x11 -> x2, local copies, waits for them, and re-layouts: 6.74 us -> 1.04 us
    ppermute x33, starting transfers between devices: 40.8 us -> 46 us  [moved(): return lax.ppermute(value, AXES, pairs)]
    reshape x2 -> x0, local copies, waits for them, and re-layouts: 3 us -> none  [gathered_amplitudes(): amplitudes.reshape(n_ij, n_d, 2, 4, 64).transpose(2, 3, 0, 1, 4)]
  transfers between devices with their start and end apart: 33 -> 33, of which waited for: 12 -> 14; matrix products, arithmetic and copies ran while one was open for 5% -> 2% of each run, Pallas kernels for 16% -> 19%
where the time goes in v2:
time: 135 us; the launch traced here: 134 us
  starting transfers between devices  46 us (34%)
  waiting for transfers between devices  44.2 us (33%)
  Pallas kernels  39.4 us (29%)
  local copies, waits for them, and re-layouts  3.15 us (2%)
    ppermute x33, starting transfers between devices, moved(): return lax.ppermute(value, AXES, pairs)  46 us
    ppermute x33, waiting for transfers between devices, moved(): return lax.ppermute(value, AXES, pairs)  44.2 us
    pallas_call x3, Pallas kernels, contracted(): pl.pallas_call(functools.partial(kernel, [len(window[j]) for j in js], le...  38.1 us
  transfers between devices with their start and end apart: 33, of which 14 were waited for; matrix products, arithmetic and copies ran while one was open for 2% of the time, Pallas kernels for 19%

profile of v2, /device:TPU:0, one launch (start us, length us, event | category | flops | bytes accessed | tf_op | source)
XLA Modules:
  0.0 134.4 jit_solution(7453762787994737278)
XLA Ops:
  1.3 3.5 %collective-permute-start.1 = (bf16[64,2048]{1,0:T(8,128)(2,1)S(1)}, bf16[64,2048]{1,0:T(8,128)(2,1)S(1)}, u32[]{:S(2)}, u32[]{:S(2)}) collective-permute-start(bf16[64,2048]{1,0:T(8,128)(2,1)S(1)} %get-tuple-element.9), channel_id=1, source_target_pairs={{0,4},{16,20},{32,36},{48,52},{64,69},{80,85},{96,101},{112,117}} | collective-permute-start | bytes 786440 | tf_op jit(solution)/shard_map/ppermute | solution.py:32
  4.8 1.9 %collective-permute-start.2 = (bf16[64,2048]{1,0:T(8,128)(2,1)S(1)}, bf16[64,2048]{1,0:T(8,128)(2,1)S(1)}, u32[]{:S(2)}, u32[]{:S(2)}) collective-permute-start(bf16[64,2048]{1,0:T(8,128)(2,1)S(1)} %get-tuple-element.11), channel_id=1, source_target_pairs={{0,12},{16,28},{32,44},{48,60},{64,77},{80,93},{96,109},{112,125}} | collective-permute-start | bytes 786440 | tf_op jit(solution)/shard_map/ppermute | solution.py:32
  15.6 5.4 %collective-permute-start.7 = (bf16[64,2048]{1,0:T(8,128)(2,1)S(1)}, bf16[64,2048]{1,0:T(8,128)(2,1)S(1)}, u32[]{:S(2)}, u32[]{:S(2)}) collective-permute-start(bf16[64,2048]{1,0:T(8,128)(2,1)S(1)} %add_add_fusion.1), channel_id=1, source_target_pairs={{0,64},{16,80},{32,96},{48,112},{65,1},{81,17},{97,33},{113,49},{4... | collective-permute-start | bytes 786440 | tf_op jit(solution)/shard_map/ppermute | solution.py:32
  25.1 3.2 %collective-permute-start.9 = (bf16[64,2048]{1,0:T(8,128)(2,1)S(1)}, bf16[64,2048]{1,0:T(8,128)(2,1)S(1)}, u32[]{:S(2)}, u32[]{:S(2)}) collective-permute-start(bf16[64,2048]{1,0:T(8,128)(2,1)S(1)} %add_add_fusion.refs_2_), channel_id=1, source_target_pairs={{0,12},{1,13},{16,28},{17,29},{32,44},{33,45},{48,60},{49,61},{2,1... | collective-permute-start | bytes 786440 | tf_op jit(solution)/shard_map/ppermute | solution.py:32
  28.3 4.0 %collective-permute-start.24 = (bf16[64,2048]{1,0:T(8,128)(2,1)S(1)}, bf16[64,2048]{1,0:T(8,128)(2,1)S(1)}, u32[]{:S(2)}, u32[]{:S(2)}) collective-permute-start(bf16[64,2048]{1,0:T(8,128)(2,1)S(1)} %add_add_fusion.refs_2_), channel_id=1, source_target_pairs={{0,48},{1,49},{16,0},{17,1},{32,16},{33,17},{48,32},{49,33},{2,50}... | collective-permute-start | bytes 786440 | tf_op jit(solution)/shard_map/ppermute | solution.py:32
  32.4 3.3 %collective-permute-done.10 = bf16[64,2048]{1,0:T(8,128)(2,1)S(1)} collective-permute-done((bf16[64,2048]{1,0:T(8,128)(2,1)S(1)}, bf16[64,2048]{1,0:T(8,128)(2,1)S(1)}, u32[]{:S(2)}, u32[]{:S(2)}) %collective-permute-start.10) | collective-permute-done | bytes 262176 | tf_op jit(solution)/shard_map/ppermute | solution.py:32
  35.7 5.2 %collective-permute-done.13 = bf16[64,2048]{1,0:T(8,128)(2,1)S(1)} collective-permute-done((bf16[64,2048]{1,0:T(8,128)(2,1)S(1)}, bf16[64,2048]{1,0:T(8,128)(2,1)S(1)}, u32[]{:S(2)}, u32[]{:S(2)}) %collective-permute-start.13) | collective-permute-done | bytes 262176 | tf_op jit(solution)/shard_map/ppermute | solution.py:32
  41.4 2.0 %collective-permute-start.26 = (bf16[64,2048]{1,0:T(8,128)(2,1)S(1)}, bf16[64,2048]{1,0:T(8,128)(2,1)S(1)}, u32[]{:S(2)}, u32[]{:S(2)}) collective-permute-start(bf16[64,2048]{1,0:T(8,128)(2,1)S(1)} %add_add_fusion.refs_2_), channel_id=1, source_target_pairs={{0,16},{1,17},{16,32},{17,33},{32,48},{33,49},{48,0},{49,1},{2,18}... | collective-permute-start | bytes 786440 | tf_op jit(solution)/shard_map/ppermute | solution.py:32
  43.4 3.6 %collective-permute-start.8 = (bf16[64,2048]{1,0:T(8,128)(2,1)S(1)}, bf16[64,2048]{1,0:T(8,128)(2,1)S(1)}, u32[]{:S(2)}, u32[]{:S(2)}) collective-permute-start(bf16[64,2048]{1,0:T(8,128)(2,1)S(1)} %add_add_fusion.refs_2_), channel_id=1, source_target_pairs={{0,32},{1,33},{16,48},{17,49},{32,0},{33,1},{48,16},{49,17},{2,34}... | collective-permute-start | bytes 786440 | tf_op jit(solution)/shard_map/ppermute | solution.py:32
  47.0 4.7 %collective-permute-done.26.refs_5_ = bf16[64,2048]{1,0:T(8,128)(2,1)S(1)} collective-permute-done((bf16[64,2048]{1,0:T(8,128)(2,1)S(1)}, bf16[64,2048]{1,0:T(8,128)(2,1)S(1)}, u32[]{:S(2)}, u32[]{:S(2)}) %collective-permute-start.26) | collective-permute-done | bytes 262176 | tf_op jit(solution)/shard_map/ppermute | solution.py:32
  51.8 2.9 %collective-permute-start.14 = (bf16[96,2048]{1,0:T(8,128)(2,1)S(1)}, bf16[96,2048]{1,0:T(8,128)(2,1)S(1)}, u32[]{:S(2)}, u32[]{:S(2)}) collective-permute-start(bf16[96,2048]{1,0:T(8,128)(2,1)S(1)} %pad_maximum_fusion.2.refs_4_), channel_id=1, source_target_pairs={{0,48},{1,49},{16,0},{17,1},{32,16},{33,17},{48,32},{49,33},{2,50}... | collective-permute-start | bytes 1179656 | tf_op jit(solution)/shard_map/ppermute | solution.py:32
  54.7 4.1 %collective-permute-done.8.refs_2_ = bf16[64,2048]{1,0:T(8,128)(2,1)S(1)} collective-permute-done((bf16[64,2048]{1,0:T(8,128)(2,1)S(1)}, bf16[64,2048]{1,0:T(8,128)(2,1)S(1)}, u32[]{:S(2)}, u32[]{:S(2)}) %collective-permute-start.8) | collective-permute-done | bytes 262176 | tf_op jit(solution)/shard_map/ppermute | solution.py:32
  58.9 3.2 %collective-permute-start.25 = (bf16[96,2048]{1,0:T(8,128)(2,1)S(1)}, bf16[96,2048]{1,0:T(8,128)(2,1)S(1)}, u32[]{:S(2)}, u32[]{:S(2)}) collective-permute-start(bf16[96,2048]{1,0:T(8,128)(2,1)S(1)} %pad_maximum_fusion.1.refs_3_), channel_id=1, source_target_pairs={{0,48},{1,49},{16,0},{17,1},{32,16},{33,17},{48,32},{49,33},{2,50}... | collective-permute-start | bytes 1179656 | tf_op jit(solution)/shard_map/ppermute | solution.py:32
  62.1 2.2 %collective-permute-done.14.refs_4_ = bf16[96,2048]{1,0:T(8,128)(2,1)S(1)} collective-permute-done((bf16[96,2048]{1,0:T(8,128)(2,1)S(1)}, bf16[96,2048]{1,0:T(8,128)(2,1)S(1)}, u32[]{:S(2)}, u32[]{:S(2)}) %collective-permute-start.14) | collective-permute-done | bytes 393248 | tf_op jit(solution)/shard_map/ppermute | solution.py:32
  65.9 6.0 %collective-permute-done.27.refs_7_ = bf16[96,2048]{1,0:T(8,128)(2,1)S(1)} collective-permute-done((bf16[96,2048]{1,0:T(8,128)(2,1)S(1)}, bf16[96,2048]{1,0:T(8,128)(2,1)S(1)}, u32[]{:S(2)}, u32[]{:S(2)}) %collective-permute-start.27) | collective-permute-done | bytes 393248 | tf_op jit(solution)/shard_map/ppermute | solution.py:32
  73.2 4.9 %collective-permute-done.11.refs_6_ = bf16[96,2048]{1,0:T(8,128)(2,1)S(1)} collective-permute-done((bf16[96,2048]{1,0:T(8,128)(2,1)S(1)}, bf16[96,2048]{1,0:T(8,128)(2,1)S(1)}, u32[]{:S(2)}, u32[]{:S(2)}) %collective-permute-start.11) | collective-permute-done | bytes 393248 | tf_op jit(solution)/shard_map/ppermute | solution.py:32
  78.1 2.1 %collective-permute-start.19 = (bf16[4,16,4096]{2,1,0:T(8,128)(2,1)S(1)}, bf16[4,16,4096]{2,1,0:T(8,128)(2,1)S(1)}, u32[]{:S(2)}, u32[]{:S(2)}) collective-permute-start(bf16[4,16,4096]{2,1,0:T(8,128)(2,1)S(1)} %collective-permute-done.17.refs_6_.refs_14_.refs_22_.refs_30_), channel_id=1, source_target_pairs={{0,12},{1,13},{16,28},{17,29},{32,44},{33,45},{48,60},{49,61},{2,1... | collective-permute-start | bytes 1572872 | tf_op jit(solution)/shard_map/ppermute | solution.py:32
  80.4 14.4 %shard_map.30.refs_38_.refs_39_ = bf16[2,256,4096]{2,1,0:T(8,128)(2,1)S(1)} custom-call(s32[5]{0:T(128)S(1)} %stack.23.pos_ref, bf16[32,64,2048]{2,1,0:T(8,128)(2,1)} %refs_0_.5, bf16[32,64,2048]{2,1,0:T(8,128)(2,1)} %collective-permute-done.refs_1_, bf16[64,2048]{1,0:T(8,128)(2,1)S(1)} %collective-permute-done.24.refs_2_, ...), custom_call_target="tpu_custom_call" | custom-call | flops 8589934592 | bytes 20971520 | tf_op jit(solution)/shard_map/pallas_call | solution.py:223
  94.9 2.0 %collective-permute-start.12 = (bf16[96,2048]{1,0:T(8,128)(2,1)S(1)}, bf16[96,2048]{1,0:T(8,128)(2,1)S(1)}, u32[]{:S(2)}, u32[]{:S(2)}) collective-permute-start(bf16[96,2048]{1,0:T(8,128)(2,1)S(1)} %collective-permute-done.11.refs_6_), channel_id=1, source_target_pairs={{0,16},{1,17},{16,32},{17,33},{32,48},{33,49},{48,0},{49,1},{2,18}... | collective-permute-start | bytes 1179656 | tf_op jit(solution)/shard_map/ppermute | solution.py:32
  96.9 10.1 %shard_map.29.refs_37_ = bf16[1,256,4096]{2,1,0:T(8,128)(2,1)S(1)} custom-call(s32[5]{0:T(128)S(1)} %stack.23.pos_ref, bf16[32,64,2048]{2,1,0:T(8,128)(2,1)} %refs_0_.5, bf16[32,64,2048]{2,1,0:T(8,128)(2,1)} %collective-permute-done.refs_1_, bf16[64,2048]{1,0:T(8,128)(2,1)S(1)} %add_add_fusion.refs_2_, bf16[96,2048]{1,0:T(8,128)(2,1)S(1)} %pad_maximum_fusion.1.refs_3_, ...), custom_call_target="tpu_custom_call" | custom-call | flops 4294967296 | bytes 20971520 | tf_op jit(solution)/shard_map/pallas_call | solution.py:223
  107.1 13.6 %shard_map.31 = f32[8,2,8,256]{3,2,1,0:T(8,128)S(1)} custom-call(s32[5]{0:T(128)S(1)} %stack.23.pos_ref, bf16[32,64,2048]{2,1,0:T(8,128)(2,1)} %refs_0_.5, bf16[32,64,2048]{2,1,0:T(8,128)(2,1)} %collective-permute-done.refs_1_, bf16[64,2048]{1,0:T(8,128)(2,1)S(1)} %collective-permute-done.8.refs_2_, bf16[96,2048]{1,0:T(8,128)(2,1)S(1)} %collective-permute-done.12.refs_3_, ...), custom_call_target="tpu_custom_call" | custom-call | flops 4294967296 | bytes 20971520 | tf_op jit(solution)/shard_map/pallas_call | solution.py:223
  122.2 5.4 %collective-permute-done.29 = f32[4,16,128]{2,1,0:T(8,128)S(1)} collective-permute-done((f32[4,16,128]{2,1,0:T(8,128)S(1)}, f32[4,16,128]{2,1,0:T(8,128)S(1)}, u32[]{:S(2)}, u32[]{:S(2)}) %collective-permute-start.29) | collective-permute-done | bytes 32800 | tf_op jit(solution)/shard_map/ppermute | solution.py:32
  127.7 2.3 %collective-permute-start.31 = (f32[16,128]{1,0:T(8,128)S(1)}, f32[16,128]{1,0:T(8,128)S(1)}, u32[]{:S(2)}, u32[]{:S(2)}) collective-permute-start(f32[16,128]{1,0:T(8,128)S(1)} %get-tuple-element.19), channel_id=1, source_target_pairs={{0,16},{1,17},{16,32},{17,33},{32,48},{33,49},{48,0},{49,1},{2,18}... | collective-permute-start | bytes 24584 | tf_op jit(solution)/shard_map/ppermute | solution.py:32
  131.0 1.8 %collective-permute-done.30 = f32[16,128]{1,0:T(8,128)S(1)} collective-permute-done((f32[16,128]{1,0:T(8,128)S(1)}, f32[16,128]{1,0:T(8,128)S(1)}, u32[]{:S(2)}, u32[]{:S(2)}) %collective-permute-start.30) | collective-permute-done | bytes 8224 | tf_op jit(solution)/shard_map/ppermute | solution.py:32
  (66 shorter events, 21.9 us)
Async XLA Ops:
  0.0 80.3 %collective-permute-start = (bf16[32,64,2048]{2,1,0:T(8,128)(2,1)}, bf16[32,64,2048]{2,1,0:T(8,128)(2,1)}, u32[]{:S(2)}, u32[]{:S(2)}) collective-permute-start(bf16[32,64,2048]{2,1,0:T(8,128)(2,1)} %refs_0_.5), channel_id=1, source_target_pairs={{0,1},{1,0},{16,17},{17,16},{32,33},{33,32},{48,49},{49,48},{2,3},... | collective-permute-start | bytes 25165832 | tf_op jit(solution)/shard_map/ppermute | solution.py:32
  1.3 7.7 %collective-permute-start.1 = (bf16[64,2048]{1,0:T(8,128)(2,1)S(1)}, bf16[64,2048]{1,0:T(8,128)(2,1)S(1)}, u32[]{:S(2)}, u32[]{:S(2)}) collective-permute-start(bf16[64,2048]{1,0:T(8,128)(2,1)S(1)} %get-tuple-element.9), channel_id=1, source_target_pairs={{0,4},{16,20},{32,36},{48,52},{64,69},{80,85},{96,101},{112,117}} | collective-permute-start | bytes 786440 | tf_op jit(solution)/shard_map/ppermute | solution.py:32
  13.0 10.6 %collective-permute-start.5 = (bf16[64,2048]{1,0:T(8,128)(2,1)S(1)}, bf16[64,2048]{1,0:T(8,128)(2,1)S(1)}, u32[]{:S(2)}, u32[]{:S(2)}) collective-permute-start(bf16[64,2048]{1,0:T(8,128)(2,1)S(1)} %add_add_fusion.1), channel_id=1, source_target_pairs={{0,2},{16,18},{32,34},{48,50},{65,67},{81,83},{97,99},{113,115},{4... | collective-permute-start | bytes 786440 | tf_op jit(solution)/shard_map/ppermute | solution.py:32
  14.3 9.2 %collective-permute-start.6 = (bf16[64,2048]{1,0:T(8,128)(2,1)S(1)}, bf16[64,2048]{1,0:T(8,128)(2,1)S(1)}, u32[]{:S(2)}, u32[]{:S(2)}) collective-permute-start(bf16[64,2048]{1,0:T(8,128)(2,1)S(1)} %add_add_fusion.1), channel_id=1, source_target_pairs={{0,66},{16,82},{32,98},{48,114},{65,3},{81,19},{97,35},{113,51},{4... | collective-permute-start | bytes 786440 | tf_op jit(solution)/shard_map/ppermute | solution.py:32
  15.6 9.3 %collective-permute-start.7 = (bf16[64,2048]{1,0:T(8,128)(2,1)S(1)}, bf16[64,2048]{1,0:T(8,128)(2,1)S(1)}, u32[]{:S(2)}, u32[]{:S(2)}) collective-permute-start(bf16[64,2048]{1,0:T(8,128)(2,1)S(1)} %add_add_fusion.1), channel_id=1, source_target_pairs={{0,64},{16,80},{32,96},{48,112},{65,1},{81,17},{97,33},{113,49},{4... | collective-permute-start | bytes 786440 | tf_op jit(solution)/shard_map/ppermute | solution.py:32
  24.9 10.8 %collective-permute-start.10 = (bf16[64,2048]{1,0:T(8,128)(2,1)S(1)}, bf16[64,2048]{1,0:T(8,128)(2,1)S(1)}, u32[]{:S(2)}, u32[]{:S(2)}) collective-permute-start(bf16[64,2048]{1,0:T(8,128)(2,1)S(1)} %add_add_fusion.refs_2_), channel_id=1, source_target_pairs={{0,8},{1,9},{16,24},{17,25},{32,40},{33,41},{48,56},{49,57},{2,10}... | collective-permute-start | bytes 786440 | tf_op jit(solution)/shard_map/ppermute | solution.py:32
  25.1 15.9 %collective-permute-start.13 = (bf16[64,2048]{1,0:T(8,128)(2,1)S(1)}, bf16[64,2048]{1,0:T(8,128)(2,1)S(1)}, u32[]{:S(2)}, u32[]{:S(2)}) collective-permute-start(bf16[64,2048]{1,0:T(8,128)(2,1)S(1)} %add_add_fusion.refs_2_), channel_id=1, source_target_pairs={{0,4},{1,5},{16,20},{17,21},{32,36},{33,37},{48,52},{49,53},{2,6},... | collective-permute-start | bytes 786440 | tf_op jit(solution)/shard_map/ppermute | solution.py:32
  25.1 16.3 %collective-permute-start.9 = (bf16[64,2048]{1,0:T(8,128)(2,1)S(1)}, bf16[64,2048]{1,0:T(8,128)(2,1)S(1)}, u32[]{:S(2)}, u32[]{:S(2)}) collective-permute-start(bf16[64,2048]{1,0:T(8,128)(2,1)S(1)} %add_add_fusion.refs_2_), channel_id=1, source_target_pairs={{0,12},{1,13},{16,28},{17,29},{32,44},{33,45},{48,60},{49,61},{2,1... | collective-permute-start | bytes 786440 | tf_op jit(solution)/shard_map/ppermute | solution.py:32
  28.3 15.1 %collective-permute-start.24 = (bf16[64,2048]{1,0:T(8,128)(2,1)S(1)}, bf16[64,2048]{1,0:T(8,128)(2,1)S(1)}, u32[]{:S(2)}, u32[]{:S(2)}) collective-permute-start(bf16[64,2048]{1,0:T(8,128)(2,1)S(1)} %add_add_fusion.refs_2_), channel_id=1, source_target_pairs={{0,48},{1,49},{16,0},{17,1},{32,16},{33,17},{48,32},{49,33},{2,50}... | collective-permute-start | bytes 786440 | tf_op jit(solution)/shard_map/ppermute | solution.py:32
  35.7 23.0 %collective-permute-start.17 = (bf16[4,16,4096]{2,1,0:T(8,128)(2,1)S(1)}, bf16[4,16,4096]{2,1,0:T(8,128)(2,1)S(1)}, u32[]{:S(2)}, u32[]{:S(2)}) collective-permute-start(bf16[4,16,4096]{2,1,0:T(8,128)(2,1)S(1)} %pad_maximum_fusion.refs_5_.refs_13_.refs_21_.refs_29_), channel_id=1, source_target_pairs={{0,2},{1,3},{16,18},{17,19},{32,34},{33,35},{48,50},{49,51},{2,0},... | collective-permute-start | bytes 1572872 | tf_op jit(solution)/shard_map/ppermute | solution.py:32
  41.0 18.0 %collective-permute-start.20 = (bf16[4,16,4096]{2,1,0:T(8,128)(2,1)S(1)}, bf16[4,16,4096]{2,1,0:T(8,128)(2,1)S(1)}, u32[]{:S(2)}, u32[]{:S(2)}) collective-permute-start(bf16[4,16,4096]{2,1,0:T(8,128)(2,1)S(1)} %pad_maximum_fusion.refs_5_.refs_13_.refs_21_.refs_29_), channel_id=1, source_target_pairs={{0,8},{1,9},{16,24},{17,25},{32,40},{33,41},{48,56},{49,57},{2,10}... | collective-permute-start | bytes 1572872 | tf_op jit(solution)/shard_map/ppermute | solution.py:32
  41.4 10.4 %collective-permute-start.26 = (bf16[64,2048]{1,0:T(8,128)(2,1)S(1)}, bf16[64,2048]{1,0:T(8,128)(2,1)S(1)}, u32[]{:S(2)}, u32[]{:S(2)}) collective-permute-start(bf16[64,2048]{1,0:T(8,128)(2,1)S(1)} %add_add_fusion.refs_2_), channel_id=1, source_target_pairs={{0,16},{1,17},{16,32},{17,33},{32,48},{33,49},{48,0},{49,1},{2,18}... | collective-permute-start | bytes 786440 | tf_op jit(solution)/shard_map/ppermute | solution.py:32
  43.4 15.4 %collective-permute-start.8 = (bf16[64,2048]{1,0:T(8,128)(2,1)S(1)}, bf16[64,2048]{1,0:T(8,128)(2,1)S(1)}, u32[]{:S(2)}, u32[]{:S(2)}) collective-permute-start(bf16[64,2048]{1,0:T(8,128)(2,1)S(1)} %add_add_fusion.refs_2_), channel_id=1, source_target_pairs={{0,32},{1,33},{16,48},{17,49},{32,0},{33,1},{48,16},{49,17},{2,34}... | collective-permute-start | bytes 786440 | tf_op jit(solution)/shard_map/ppermute | solution.py:32
  51.8 12.5 %collective-permute-start.14 = (bf16[96,2048]{1,0:T(8,128)(2,1)S(1)}, bf16[96,2048]{1,0:T(8,128)(2,1)S(1)}, u32[]{:S(2)}, u32[]{:S(2)}) collective-permute-start(bf16[96,2048]{1,0:T(8,128)(2,1)S(1)} %pad_maximum_fusion.2.refs_4_), channel_id=1, source_target_pairs={{0,48},{1,49},{16,0},{17,1},{32,16},{33,17},{48,32},{49,33},{2,50}... | collective-permute-start | bytes 1179656 | tf_op jit(solution)/shard_map/ppermute | solution.py:32
  58.8 13.2 %collective-permute-start.27 = (bf16[96,2048]{1,0:T(8,128)(2,1)S(1)}, bf16[96,2048]{1,0:T(8,128)(2,1)S(1)}, u32[]{:S(2)}, u32[]{:S(2)}) collective-permute-start(bf16[96,2048]{1,0:T(8,128)(2,1)S(1)} %pad_maximum_fusion.2.refs_4_), channel_id=1, source_target_pairs={{0,16},{1,17},{16,32},{17,33},{32,48},{33,49},{48,0},{49,1},{2,18}... | collective-permute-start | bytes 1179656 | tf_op jit(solution)/shard_map/ppermute | solution.py:32
  58.8 19.4 %collective-permute-start.11 = (bf16[96,2048]{1,0:T(8,128)(2,1)S(1)}, bf16[96,2048]{1,0:T(8,128)(2,1)S(1)}, u32[]{:S(2)}, u32[]{:S(2)}) collective-permute-start(bf16[96,2048]{1,0:T(8,128)(2,1)S(1)} %pad_maximum_fusion.1.refs_3_), channel_id=1, source_target_pairs={{0,16},{1,17},{16,32},{17,33},{32,48},{33,49},{48,0},{49,1},{2,18}... | collective-permute-start | bytes 1179656 | tf_op jit(solution)/shard_map/ppermute | solution.py:32
  58.9 21.4 %collective-permute-start.25 = (bf16[96,2048]{1,0:T(8,128)(2,1)S(1)}, bf16[96,2048]{1,0:T(8,128)(2,1)S(1)}, u32[]{:S(2)}, u32[]{:S(2)}) collective-permute-start(bf16[96,2048]{1,0:T(8,128)(2,1)S(1)} %pad_maximum_fusion.1.refs_3_), channel_id=1, source_target_pairs={{0,48},{1,49},{16,0},{17,1},{32,16},{33,17},{48,32},{49,33},{2,50}... | collective-permute-start | bytes 1179656 | tf_op jit(solution)/shard_map/ppermute | solution.py:32
  64.3 30.5 %collective-permute-start.18 = (bf16[4,16,4096]{2,1,0:T(8,128)(2,1)S(1)}, bf16[4,16,4096]{2,1,0:T(8,128)(2,1)S(1)}, u32[]{:S(2)}, u32[]{:S(2)}) collective-permute-start(bf16[4,16,4096]{2,1,0:T(8,128)(2,1)S(1)} %pad_maximum_fusion.refs_5_.refs_13_.refs_21_.refs_29_), channel_id=1, source_target_pairs={{0,12},{1,13},{16,28},{17,29},{32,44},{33,45},{48,60},{49,61},{2,1... | collective-permute-start | bytes 1572872 | tf_op jit(solution)/shard_map/ppermute | solution.py:32
  72.0 22.9 %collective-permute-start.22 = (bf16[4,16,4096]{2,1,0:T(8,128)(2,1)S(1)}, bf16[4,16,4096]{2,1,0:T(8,128)(2,1)S(1)}, u32[]{:S(2)}, u32[]{:S(2)}) collective-permute-start(bf16[4,16,4096]{2,1,0:T(8,128)(2,1)S(1)} %pad_maximum_fusion.refs_5_.refs_13_.refs_21_.refs_29_), channel_id=1, source_target_pairs={{0,4},{1,5},{16,20},{17,21},{32,36},{33,37},{48,52},{49,53},{2,6},... | collective-permute-start | bytes 1572872 | tf_op jit(solution)/shard_map/ppermute | solution.py:32
  78.1 28.9 %collective-permute-start.19 = (bf16[4,16,4096]{2,1,0:T(8,128)(2,1)S(1)}, bf16[4,16,4096]{2,1,0:T(8,128)(2,1)S(1)}, u32[]{:S(2)}, u32[]{:S(2)}) collective-permute-start(bf16[4,16,4096]{2,1,0:T(8,128)(2,1)S(1)} %collective-permute-done.17.refs_6_.refs_14_.refs_22_.refs_30_), channel_id=1, source_target_pairs={{0,12},{1,13},{16,28},{17,29},{32,44},{33,45},{48,60},{49,61},{2,1... | collective-permute-start | bytes 1572872 | tf_op jit(solution)/shard_map/ppermute | solution.py:32
  80.3 26.8 %collective-permute-start.23 = (bf16[4,16,4096]{2,1,0:T(8,128)(2,1)S(1)}, bf16[4,16,4096]{2,1,0:T(8,128)(2,1)S(1)}, u32[]{:S(2)}, u32[]{:S(2)}) collective-permute-start(bf16[4,16,4096]{2,1,0:T(8,128)(2,1)S(1)} %collective-permute-done.17.refs_6_.refs_14_.refs_22_.refs_30_), channel_id=1, source_target_pairs={{0,4},{1,5},{16,20},{17,21},{32,36},{33,37},{48,52},{49,53},{2,6},... | collective-permute-start | bytes 1572872 | tf_op jit(solution)/shard_map/ppermute | solution.py:32
  80.3 26.7 %collective-permute-start.21 = (bf16[4,16,4096]{2,1,0:T(8,128)(2,1)S(1)}, bf16[4,16,4096]{2,1,0:T(8,128)(2,1)S(1)}, u32[]{:S(2)}, u32[]{:S(2)}) collective-permute-start(bf16[4,16,4096]{2,1,0:T(8,128)(2,1)S(1)} %collective-permute-done.20.refs_9_.refs_17_.refs_25_.refs_33_), channel_id=1, source_target_pairs={{0,2},{1,3},{16,18},{17,19},{32,34},{33,35},{48,50},{49,51},{2,0},... | collective-permute-start | bytes 1572872 | tf_op jit(solution)/shard_map/ppermute | solution.py:32
  94.8 12.2 %collective-permute-start.15 = (bf16[96,2048]{1,0:T(8,128)(2,1)S(1)}, bf16[96,2048]{1,0:T(8,128)(2,1)S(1)}, u32[]{:S(2)}, u32[]{:S(2)}) collective-permute-start(bf16[96,2048]{1,0:T(8,128)(2,1)S(1)} %collective-permute-done.14.refs_4_), channel_id=1, source_target_pairs={{0,48},{1,49},{16,0},{17,1},{32,16},{33,17},{48,32},{49,33},{2,50}... | collective-permute-start | bytes 1179656 | tf_op jit(solution)/shard_map/ppermute | solution.py:32
  94.9 12.1 %collective-permute-start.12 = (bf16[96,2048]{1,0:T(8,128)(2,1)S(1)}, bf16[96,2048]{1,0:T(8,128)(2,1)S(1)}, u32[]{:S(2)}, u32[]{:S(2)}) collective-permute-start(bf16[96,2048]{1,0:T(8,128)(2,1)S(1)} %collective-permute-done.11.refs_6_), channel_id=1, source_target_pairs={{0,16},{1,17},{16,32},{17,33},{32,48},{33,49},{48,0},{49,1},{2,18}... | collective-permute-start | bytes 1179656 | tf_op jit(solution)/shard_map/ppermute | solution.py:32
  (10 other events, 41.7 us)
